TPU v7x, 128 devices: a whole 4x4x4 slice. The times are simulated.
128 devices in a mesh: dp: 1, row: 16 (over z, y), col: 8 (over x, core).
Axes of the slice: x: 4, y: 4, z: 4, core: 2. Of those that a mesh axis runs over, the one named last changes fastest.
Arguments:
- pair_rep: bfloat16 [768, 768, 64], P(('dp', 'row'), 'col')
- res_mask: int32 [768], P('dp')
- ln_gamma: float32 [64], replicated
- ln_beta: float32 [64], replicated
- w_q: bfloat16 [64, 64], replicated
- w_k: bfloat16 [64, 64], replicated
- w_v: bfloat16 [64, 64], replicated
- w_b: bfloat16 [64, 4], replicated
- w_g: bfloat16 [64, 64], replicated
- w_o: bfloat16 [64, 64], replicated
Outputs:
- output: bfloat16 [768, 768, 64], P(('dp', 'row'), 'col')
All inputs are finite; a program needn't handle non-finite values.
Results may differ from a plain program's by a relative error of at most 0.00749946.
Values are sent between devices in bfloat16 or wider.
A program may use at most 1 GiB of HBM per device.

v0:
```python
import jax
import jax.numpy as jnp
from jax import lax
from jax.sharding import PartitionSpec as P, NamedSharding

LN_EPS = 1e-5


def layer_norm(pair_rep, ln_gamma, ln_beta):
    pair_f32 = pair_rep.astype(jnp.float32)
    mean_c = jnp.mean(pair_f32, axis=-1, keepdims=True)
    centered = pair_f32 - mean_c
    var_c = jnp.mean(jnp.square(centered), axis=-1, keepdims=True)
    return (centered * lax.rsqrt(var_c + LN_EPS) * ln_gamma + ln_beta).astype(jnp.bfloat16)


def solution(mesh):
    col_size = mesh.shape['col']
    shift_pairs = [(src_dev, (src_dev + 1) % col_size) for src_dev in range(col_size)]
    tile_spec = P(('dp', 'row'), 'col', None)

    def per_device(pair_tile, res_mask, ln_gamma, ln_beta, w_q, w_k, w_v, w_b, w_g, w_o):
        row_len, col_len, chan_dim = pair_tile.shape
        num_heads = w_b.shape[1]
        head_dim = w_q.shape[1] // num_heads
        col_idx = lax.axis_index('col')
        normed = layer_norm(pair_tile, ln_gamma, ln_beta)
        head_shape = (row_len, col_len, num_heads, head_dim)
        queries = (jnp.dot(normed, w_q, preferred_element_type=jnp.float32) * head_dim ** -0.5).astype(jnp.bfloat16).reshape(head_shape)
        key_blk = jnp.dot(normed, w_k, preferred_element_type=jnp.float32).astype(jnp.bfloat16).reshape(head_shape)
        val_blk = jnp.dot(normed, w_v, preferred_element_type=jnp.float32).astype(jnp.bfloat16).reshape(head_shape)
        gate_vals = jax.nn.sigmoid(jnp.dot(normed, w_g, preferred_element_type=jnp.float32))
        bias_tile = jnp.dot(normed, w_b, preferred_element_type=jnp.float32).astype(jnp.bfloat16)
        bias_cols = lax.all_gather(bias_tile, 'row', axis=0, tiled=True)
        bias_rows = lax.all_to_all(bias_cols, 'col', 0, 1, tiled=True)
        key_bias = jnp.where(res_mask > 0, 0.0, -1e9).astype(jnp.float32)
        full_bias = jnp.transpose(bias_rows, (2, 0, 1)).astype(jnp.float32) + key_bias

        def fold_block(fold_state, key_part, val_part, src_col):
            run_max, run_sum, acc_out = fold_state
            bias_part = lax.dynamic_slice_in_dim(full_bias, src_col * col_len, col_len, axis=2)
            logits = jnp.einsum('ijhd,ikhd->ihjk', queries, key_part, preferred_element_type=jnp.float32) + bias_part
            new_max = jnp.maximum(run_max, jnp.max(logits, axis=-1))
            rescale = jnp.exp(run_max - new_max)
            weights = jnp.exp(logits - new_max[..., None])
            run_sum = run_sum * rescale + jnp.sum(weights, axis=-1)
            acc_out = acc_out * rescale[..., None] + jnp.einsum('ihjk,ikhd->ihjd', weights.astype(jnp.bfloat16), val_part, preferred_element_type=jnp.float32)
            return new_max, run_sum, acc_out

        stat_shape = (row_len, num_heads, col_len)
        init_state = (jnp.full(stat_shape, -jnp.inf, jnp.float32), jnp.zeros(stat_shape, jnp.float32), jnp.zeros(stat_shape + (head_dim,), jnp.float32))
        first_state = fold_block(init_state, key_blk, val_blk, col_idx)

        def hop_step(hop_idx, loop_state):
            kv_blocks, fold_state = loop_state
            kv_blocks = lax.ppermute(kv_blocks, 'col', shift_pairs)
            src_col = (col_idx + col_size - hop_idx) % col_size
            return kv_blocks, fold_block(fold_state, kv_blocks[0], kv_blocks[1], src_col)

        final_state = lax.fori_loop(1, col_size, hop_step, ((key_blk, val_blk), first_state))
        run_sum = final_state[1][1]
        acc_out = final_state[1][2]
        attended = jnp.transpose(acc_out / run_sum[..., None], (0, 2, 1, 3)).reshape(row_len, col_len, num_heads * head_dim)
        gated_out = (gate_vals * attended).astype(jnp.bfloat16)
        update = jnp.dot(gated_out, w_o, preferred_element_type=jnp.float32)
        return (pair_tile.astype(jnp.float32) + update).astype(jnp.bfloat16)

    return jax.shard_map(per_device, mesh=mesh, in_specs=(tile_spec, P('dp'), P(), P(), P(), P(), P(), P(), P(), P()), out_specs=tile_spec, check_vma=False)
```

profile of v0, /device:TPU:0, one launch (start us, length us, event | category | flops | bytes accessed | tf_op | source)
XLA Modules:
  0.0 225.4 jit_solution(3665743757989849733)
XLA Ops:
  3.6 26.1 %all_gather.3 = bf16[768,96,4]{1,2,0:T(4,128)(2,1)} all-gather(bf16[48,96,4]{1,2,0:T(4,128)(2,1)S(1)} %convolution_convert_fusion.2), channel_id=1, replica_groups=mesh['dp'=1,'row'=16,'col'=8] {'row'}, dimensions={0}, use_global_device_ids=true | all-gather | bytes 626688 | tf_op jit(solution)/shard_map/all_gather | solution.py:34
  29.7 4.4 %all-to-all-start = ((bf16[768,96,4]{1,2,0:T(4,128)(2,1)}), bf16[768,96,4]{1,2,0:T(4,128)(2,1)S(1)}, u32[]{:S(2)}, u32[]{:S(2)}) async-start(bf16[768,96,4]{1,2,0:T(4,128)(2,1)} %all_gather.3), calls=%async_computation | async-start | bytes 1572864 | tf_op jit(solution)/shard_map/all_to_all | solution.py:35
  38.1 9.2 %all-to-all-done = bf16[768,96,4]{1,2,0:T(4,128)(2,1)S(1)} async-done(((bf16[768,96,4]{1,2,0:T(4,128)(2,1)}), bf16[768,96,4]{1,2,0:T(4,128)(2,1)S(1)}, u32[]{:S(2)}, u32[]{:S(2)}) %all-to-all-start) | async-done | bytes 589856 | tf_op jit(solution)/shard_map/all_to_all | solution.py:35
  48.3 3.8 %add_reduce_fusion.1 = (f32[48,4,96]{2,1,0:T(4,128)S(1)}, f32[48,4,96,96]{2,3,1,0:T(8,128)S(1)}) fusion(f32[4,96,96]{1,2,0:T(8,128)S(1)} %dynamic-slice_bitcast_fusion, bf16[48,96,4,16]{1,3,2,0:T(8,128)(2,1)} %bitcast.6, bf16[48,96,4,16]{1,3,2,0:T(8,128)(2,1)} %bitcast.2), kind=kOutput, calls=%fused_computation.12 | convolution fusion | flops 60143616 | bytes 8478720 | tf_op jit(solution)/shard_map/ijhd,ikhd->ihjk/dot_general | solution.py:42
  52.2 2.7 %fusion.9 = f32[48,4,96]{2,1,0:T(4,128)S(1)} fusion(f32[48,4,96,96]{2,3,1,0:T(8,128)S(1)} %get-tuple-element.256, f32[48,4,96]{2,1,0:T(4,128)S(1)} %get-tuple-element.327, f32[4,96,96]{1,2,0:T(8,128)S(1)} %dynamic-slice_bitcast_fusion), kind=kLoop, calls=%fused_computation.14 | loop fusion | flops 5289984 | bytes 7372800 | tf_op jit(solution)/shard_map/reduce_sum | solution.py:46
  56.5 165.3 %while.23 = (s32[]{:T(128)}, bf16[48,96,4,16]{1,3,2,0:T(8,128)(2,1)}, bf16[48,96,4,16]{1,3,2,0:T(8,128)(2,1)}, f32[48,4,96]{2,1,0:T(4,128)S(1)}, f32[48,4,96]{2,...) while((s32[]{:T(128)}, ...), condition=%wide.region_7.8_spmd, body=%wide.region_4.7_spmd.sunk | while | flops 128028688 | bytes 34357640 | solution.py:60
  58.3 11.0 %collective-permute-done = bf16[48,96,4,16]{1,3,2,0:T(8,128)(2,1)S(1)} collective-permute-done((bf16[48,96,4,16]{1,3,2,0:T(8,128)(2,1)}, bf16[48,96,4,16]{1,3,2,0:T(8,128)(2,1)S(1)}, u32[]{:S(2)}, u32[]{:S(2)}) %collective-permute-start) | collective-permute-done | bytes 589856 | tf_op jit(solution)/shard_map/while/body/eval_jaxpr/ppermute | solution.py:56
  69.3 3.1 %add_reduce_fusion.3 = (f32[48,4,96]{2,1,0:T(4,128)S(1)}, f32[48,4,96,96]{2,3,1,0:T(8,128)S(1)}) fusion(f32[4,96,96]{1,2,0:T(8,128)S(1)} %constant_dynamic-slice_fusion.2, bf16[48,96,4,16]{1,3,2,0:T(8,128)(2,1)} %get-tuple-element.360, bf16[48,96,4,16]{1,3,2,0:T(8,128)(2,1)S(1)} %collective-permute-done), kind=kOutput, calls=%fused_computation.1.clone.1 | convolution fusion | flops 60143616 | bytes 8478720 | tf_op jit(solution)/shard_map/while/body/eval_jaxpr/ijhd,ikhd->ihjk/dot_general | solution.py:42
  72.5 2.7 %fusion.53 = f32[48,4,96]{2,1,0:T(4,128)S(1)} fusion(f32[48,4,96,96]{2,3,1,0:T(8,128)S(1)} %get-tuple-element.321, f32[48,4,96]{2,1,0:T(4,128)S(1)} %max.11, f32[4,96,96]{1,2,0:T(8,128)S(1)} %constant_dynamic-slice_fusion.2), kind=kLoop, calls=%fused_computation.3.clone.1 | loop fusion | flops 5289984 | bytes 7372800 | tf_op jit(solution)/shard_map/while/body/eval_jaxpr/reduce_sum | solution.py:46
  81.3 11.6 %collective-permute-done = bf16[48,96,4,16]{1,3,2,0:T(8,128)(2,1)S(1)} collective-permute-done((bf16[48,96,4,16]{1,3,2,0:T(8,128)(2,1)}, bf16[48,96,4,16]{1,3,2,0:T(8,128)(2,1)S(1)}, u32[]{:S(2)}, u32[]{:S(2)}) %collective-permute-start) | collective-permute-done | bytes 589856 | tf_op jit(solution)/shard_map/while/body/eval_jaxpr/ppermute | solution.py:56
  92.9 3.1 %add_reduce_fusion.3 = (f32[48,4,96]{2,1,0:T(4,128)S(1)}, f32[48,4,96,96]{2,3,1,0:T(8,128)S(1)}) fusion(f32[4,96,96]{1,2,0:T(8,128)S(1)} %constant_dynamic-slice_fusion.2, bf16[48,96,4,16]{1,3,2,0:T(8,128)(2,1)} %get-tuple-element.360, bf16[48,96,4,16]{1,3,2,0:T(8,128)(2,1)S(1)} %collective-permute-done), kind=kOutput, calls=%fused_computation.1.clone.1 | convolution fusion | flops 60143616 | bytes 8478720 | tf_op jit(solution)/shard_map/while/body/eval_jaxpr/ijhd,ikhd->ihjk/dot_general | solution.py:42
  96.1 2.7 %fusion.53 = f32[48,4,96]{2,1,0:T(4,128)S(1)} fusion(f32[48,4,96,96]{2,3,1,0:T(8,128)S(1)} %get-tuple-element.321, f32[48,4,96]{2,1,0:T(4,128)S(1)} %max.11, f32[4,96,96]{1,2,0:T(8,128)S(1)} %constant_dynamic-slice_fusion.2), kind=kLoop, calls=%fused_computation.3.clone.1 | loop fusion | flops 5289984 | bytes 7372800 | tf_op jit(solution)/shard_map/while/body/eval_jaxpr/reduce_sum | solution.py:46
  104.9 11.6 %collective-permute-done = bf16[48,96,4,16]{1,3,2,0:T(8,128)(2,1)S(1)} collective-permute-done((bf16[48,96,4,16]{1,3,2,0:T(8,128)(2,1)}, bf16[48,96,4,16]{1,3,2,0:T(8,128)(2,1)S(1)}, u32[]{:S(2)}, u32[]{:S(2)}) %collective-permute-start) | collective-permute-done | bytes 589856 | tf_op jit(solution)/shard_map/while/body/eval_jaxpr/ppermute | solution.py:56
  116.5 3.1 %add_reduce_fusion.3 = (f32[48,4,96]{2,1,0:T(4,128)S(1)}, f32[48,4,96,96]{2,3,1,0:T(8,128)S(1)}) fusion(f32[4,96,96]{1,2,0:T(8,128)S(1)} %constant_dynamic-slice_fusion.2, bf16[48,96,4,16]{1,3,2,0:T(8,128)(2,1)} %get-tuple-element.360, bf16[48,96,4,16]{1,3,2,0:T(8,128)(2,1)S(1)} %collective-permute-done), kind=kOutput, calls=%fused_computation.1.clone.1 | convolution fusion | flops 60143616 | bytes 8478720 | tf_op jit(solution)/shard_map/while/body/eval_jaxpr/ijhd,ikhd->ihjk/dot_general | solution.py:42
  128.5 11.6 %collective-permute-done = bf16[48,96,4,16]{1,3,2,0:T(8,128)(2,1)S(1)} collective-permute-done((bf16[48,96,4,16]{1,3,2,0:T(8,128)(2,1)}, bf16[48,96,4,16]{1,3,2,0:T(8,128)(2,1)S(1)}, u32[]{:S(2)}, u32[]{:S(2)}) %collective-permute-start) | collective-permute-done | bytes 589856 | tf_op jit(solution)/shard_map/while/body/eval_jaxpr/ppermute | solution.py:56
  140.1 3.1 %add_reduce_fusion.3 = (f32[48,4,96]{2,1,0:T(4,128)S(1)}, f32[48,4,96,96]{2,3,1,0:T(8,128)S(1)}) fusion(f32[4,96,96]{1,2,0:T(8,128)S(1)} %constant_dynamic-slice_fusion.2, bf16[48,96,4,16]{1,3,2,0:T(8,128)(2,1)} %get-tuple-element.360, bf16[48,96,4,16]{1,3,2,0:T(8,128)(2,1)S(1)} %collective-permute-done), kind=kOutput, calls=%fused_computation.1.clone.1 | convolution fusion | flops 60143616 | bytes 8478720 | tf_op jit(solution)/shard_map/while/body/eval_jaxpr/ijhd,ikhd->ihjk/dot_general | solution.py:42
  152.1 11.6 %collective-permute-done = bf16[48,96,4,16]{1,3,2,0:T(8,128)(2,1)S(1)} collective-permute-done((bf16[48,96,4,16]{1,3,2,0:T(8,128)(2,1)}, bf16[48,96,4,16]{1,3,2,0:T(8,128)(2,1)S(1)}, u32[]{:S(2)}, u32[]{:S(2)}) %collective-permute-start) | collective-permute-done | bytes 589856 | tf_op jit(solution)/shard_map/while/body/eval_jaxpr/ppermute | solution.py:56
  163.7 3.1 %add_reduce_fusion.3 = (f32[48,4,96]{2,1,0:T(4,128)S(1)}, f32[48,4,96,96]{2,3,1,0:T(8,128)S(1)}) fusion(f32[4,96,96]{1,2,0:T(8,128)S(1)} %constant_dynamic-slice_fusion.2, bf16[48,96,4,16]{1,3,2,0:T(8,128)(2,1)} %get-tuple-element.360, bf16[48,96,4,16]{1,3,2,0:T(8,128)(2,1)S(1)} %collective-permute-done), kind=kOutput, calls=%fused_computation.1.clone.1 | convolution fusion | flops 60143616 | bytes 8478720 | tf_op jit(solution)/shard_map/while/body/eval_jaxpr/ijhd,ikhd->ihjk/dot_general | solution.py:42
  166.8 2.7 %fusion.53 = f32[48,4,96]{2,1,0:T(4,128)S(1)} fusion(f32[48,4,96,96]{2,3,1,0:T(8,128)S(1)} %get-tuple-element.321, f32[48,4,96]{2,1,0:T(4,128)S(1)} %max.11, f32[4,96,96]{1,2,0:T(8,128)S(1)} %constant_dynamic-slice_fusion.2), kind=kLoop, calls=%fused_computation.3.clone.1 | loop fusion | flops 5289984 | bytes 7372800 | tf_op jit(solution)/shard_map/while/body/eval_jaxpr/reduce_sum | solution.py:46
  175.7 11.6 %collective-permute-done = bf16[48,96,4,16]{1,3,2,0:T(8,128)(2,1)S(1)} collective-permute-done((bf16[48,96,4,16]{1,3,2,0:T(8,128)(2,1)}, bf16[48,96,4,16]{1,3,2,0:T(8,128)(2,1)S(1)}, u32[]{:S(2)}, u32[]{:S(2)}) %collective-permute-start) | collective-permute-done | bytes 589856 | tf_op jit(solution)/shard_map/while/body/eval_jaxpr/ppermute | solution.py:56
  187.3 3.1 %add_reduce_fusion.3 = (f32[48,4,96]{2,1,0:T(4,128)S(1)}, f32[48,4,96,96]{2,3,1,0:T(8,128)S(1)}) fusion(f32[4,96,96]{1,2,0:T(8,128)S(1)} %constant_dynamic-slice_fusion.2, bf16[48,96,4,16]{1,3,2,0:T(8,128)(2,1)} %get-tuple-element.360, bf16[48,96,4,16]{1,3,2,0:T(8,128)(2,1)S(1)} %collective-permute-done), kind=kOutput, calls=%fused_computation.1.clone.1 | convolution fusion | flops 60143616 | bytes 8478720 | tf_op jit(solution)/shard_map/while/body/eval_jaxpr/ijhd,ikhd->ihjk/dot_general | solution.py:42
  199.3 11.6 %collective-permute-done = bf16[48,96,4,16]{1,3,2,0:T(8,128)(2,1)S(1)} collective-permute-done((bf16[48,96,4,16]{1,3,2,0:T(8,128)(2,1)}, bf16[48,96,4,16]{1,3,2,0:T(8,128)(2,1)S(1)}, u32[]{:S(2)}, u32[]{:S(2)}) %collective-permute-start) | collective-permute-done | bytes 589856 | tf_op jit(solution)/shard_map/while/body/eval_jaxpr/ppermute | solution.py:56
  210.9 3.1 %add_reduce_fusion.3 = (f32[48,4,96]{2,1,0:T(4,128)S(1)}, f32[48,4,96,96]{2,3,1,0:T(8,128)S(1)}) fusion(f32[4,96,96]{1,2,0:T(8,128)S(1)} %constant_dynamic-slice_fusion.2, bf16[48,96,4,16]{1,3,2,0:T(8,128)(2,1)} %get-tuple-element.360, bf16[48,96,4,16]{1,3,2,0:T(8,128)(2,1)S(1)} %collective-permute-done), kind=kOutput, calls=%fused_computation.1.clone.1 | convolution fusion | flops 60143616 | bytes 8478720 | tf_op jit(solution)/shard_map/while/body/eval_jaxpr/ijhd,ikhd->ihjk/dot_general | solution.py:42
  214.0 2.7 %fusion.53 = f32[48,4,96]{2,1,0:T(4,128)S(1)} fusion(f32[48,4,96,96]{2,3,1,0:T(8,128)S(1)} %get-tuple-element.321, f32[48,4,96]{2,1,0:T(4,128)S(1)} %max.11, f32[4,96,96]{1,2,0:T(8,128)S(1)} %constant_dynamic-slice_fusion.2), kind=kLoop, calls=%fused_computation.3.clone.1 | loop fusion | flops 5289984 | bytes 7372800 | tf_op jit(solution)/shard_map/while/body/eval_jaxpr/reduce_sum | solution.py:46
  (122 shorter events, 65.1 us)
Async XLA Ops:
  0.0 34.2 %copy-start = (bf16[64,64]{1,0:T(8,128)(2,1)S(1)}, bf16[64,64]{1,0:T(8,128)(2,1)}, u32[]{:S(2)}) copy-start(bf16[64,64]{1,0:T(8,128)(2,1)} %param.17) | copy-start | bytes 24580
  0.0 2.9 %copy-start.3 = (bf16[48,96,64]{1,2,0:T(8,128)(2,1)S(1)}, bf16[48,96,64]{1,2,0:T(8,128)(2,1)}, u32[]{:S(2)}) copy-start(bf16[48,96,64]{1,2,0:T(8,128)(2,1)} %param.12) | copy-start | bytes 1769476
  0.0 2.9 %copy-start.13 = (f32[64]{0:T(128)S(1)}, f32[64]{0:T(128)}, u32[]{:S(2)}) copy-start(f32[64]{0:T(128)} %param.14) | copy-start | bytes 772
  0.0 2.9 %copy-start.12 = (f32[64]{0:T(128)S(1)}, f32[64]{0:T(128)}, u32[]{:S(2)}) copy-start(f32[64]{0:T(128)} %param.15) | copy-start | bytes 772
  0.0 3.4 %copy-start.11 = (bf16[64,4]{0,1:T(4,128)(2,1)S(1)}, bf16[64,4]{0,1:T(4,128)(2,1)}, u32[]{:S(2)}) copy-start(bf16[64,4]{0,1:T(4,128)(2,1)} %param.19) | copy-start | bytes 1540
  3.4 33.4 %copy-start.1 = (bf16[48,96,64]{1,2,0:T(8,128)(2,1)}, bf16[48,96,64]{1,2,0:T(8,128)(2,1)S(1)}, u32[]{:S(2)}) copy-start(bf16[48,96,64]{1,2,0:T(8,128)(2,1)S(1)} %fusion.19) | copy-start | bytes 1769476
  3.4 30.7 %copy-start.10 = (s32[768]{0:T(1024)S(1)}, s32[768]{0:T(1024)}, u32[]{:S(2)}) copy-start(s32[768]{0:T(1024)} %param.13) | copy-start | bytes 9220
  29.7 5.8 %copy-start.7 = (bf16[64,64]{1,0:T(8,128)(2,1)S(1)}, bf16[64,64]{1,0:T(8,128)(2,1)}, u32[]{:S(2)}) copy-start(bf16[64,64]{1,0:T(8,128)(2,1)} %param.16) | copy-start | bytes 24580
  29.7 17.6 %all-to-all-start = ((bf16[768,96,4]{1,2,0:T(4,128)(2,1)}), bf16[768,96,4]{1,2,0:T(4,128)(2,1)S(1)}, u32[]{:S(2)}, u32[]{:S(2)}) async-start(bf16[768,96,4]{1,2,0:T(4,128)(2,1)} %all_gather.3), calls=%async_computation | async-start | bytes 1572864 | tf_op jit(solution)/shard_map/all_to_all | solution.py:35
  48.3 3.9 %copy-start.5 = (f32[96,768,4]{0,1,2:T(8,128)}, f32[96,768,4]{0,1,2:T(8,128)S(1)}, u32[]{:S(2)}) copy-start(f32[96,768,4]{0,1,2:T(8,128)S(1)} %bitcast_add_fusion) | copy-start | bytes 3538948
  56.7 12.6 %collective-permute-start = (bf16[48,96,4,16]{1,3,2,0:T(8,128)(2,1)}, bf16[48,96,4,16]{1,3,2,0:T(8,128)(2,1)S(1)}, u32[]{:S(2)}, u32[]{:S(2)}) collective-permute-start(bf16[48,96,4,16]{1,3,2,0:T(8,128)(2,1)} %get-tuple-element.340), channel_id=1, source_target_pairs={{0,1},{1,2},{2,3},{3,4},{4,5},{5,6},{6,7},{7,0},{8,9},{9,10},{10,1... | collective-permute-start | bytes 1769480 | tf_op jit(solution)/shard_map/while/body/eval_jaxpr/ppermute | solution.py:56
  56.7 21.0 %collective-permute-start.1 = (bf16[48,96,4,16]{1,3,2,0:T(8,128)(2,1)}, bf16[48,96,4,16]{1,3,2,0:T(8,128)(2,1)S(1)}, u32[]{:S(2)}, u32[]{:S(2)}) collective-permute-start(bf16[48,96,4,16]{1,3,2,0:T(8,128)(2,1)} %get-tuple-element.341), channel_id=1, source_target_pairs={{0,1},{1,2},{2,3},{3,4},{4,5},{5,6},{6,7},{7,0},{8,9},{9,10},{10,1... | collective-permute-start | bytes 1769480 | tf_op jit(solution)/shard_map/while/body/eval_jaxpr/ppermute | solution.py:56
  80.3 12.6 %collective-permute-start = (bf16[48,96,4,16]{1,3,2,0:T(8,128)(2,1)}, bf16[48,96,4,16]{1,3,2,0:T(8,128)(2,1)S(1)}, u32[]{:S(2)}, u32[]{:S(2)}) collective-permute-start(bf16[48,96,4,16]{1,3,2,0:T(8,128)(2,1)} %get-tuple-element.340), channel_id=1, source_target_pairs={{0,1},{1,2},{2,3},{3,4},{4,5},{5,6},{6,7},{7,0},{8,9},{9,10},{10,1... | collective-permute-start | bytes 1769480 | tf_op jit(solution)/shard_map/while/body/eval_jaxpr/ppermute | solution.py:56
  80.3 21.0 %collective-permute-start.1 = (bf16[48,96,4,16]{1,3,2,0:T(8,128)(2,1)}, bf16[48,96,4,16]{1,3,2,0:T(8,128)(2,1)S(1)}, u32[]{:S(2)}, u32[]{:S(2)}) collective-permute-start(bf16[48,96,4,16]{1,3,2,0:T(8,128)(2,1)} %get-tuple-element.341), channel_id=1, source_target_pairs={{0,1},{1,2},{2,3},{3,4},{4,5},{5,6},{6,7},{7,0},{8,9},{9,10},{10,1... | collective-permute-start | bytes 1769480 | tf_op jit(solution)/shard_map/while/body/eval_jaxpr/ppermute | solution.py:56
  103.9 12.6 %collective-permute-start = (bf16[48,96,4,16]{1,3,2,0:T(8,128)(2,1)}, bf16[48,96,4,16]{1,3,2,0:T(8,128)(2,1)S(1)}, u32[]{:S(2)}, u32[]{:S(2)}) collective-permute-start(bf16[48,96,4,16]{1,3,2,0:T(8,128)(2,1)} %get-tuple-element.340), channel_id=1, source_target_pairs={{0,1},{1,2},{2,3},{3,4},{4,5},{5,6},{6,7},{7,0},{8,9},{9,10},{10,1... | collective-permute-start | bytes 1769480 | tf_op jit(solution)/shard_map/while/body/eval_jaxpr/ppermute | solution.py:56
  103.9 21.0 %collective-permute-start.1 = (bf16[48,96,4,16]{1,3,2,0:T(8,128)(2,1)}, bf16[48,96,4,16]{1,3,2,0:T(8,128)(2,1)S(1)}, u32[]{:S(2)}, u32[]{:S(2)}) collective-permute-start(bf16[48,96,4,16]{1,3,2,0:T(8,128)(2,1)} %get-tuple-element.341), channel_id=1, source_target_pairs={{0,1},{1,2},{2,3},{3,4},{4,5},{5,6},{6,7},{7,0},{8,9},{9,10},{10,1... | collective-permute-start | bytes 1769480 | tf_op jit(solution)/shard_map/while/body/eval_jaxpr/ppermute | solution.py:56
  127.5 12.6 %collective-permute-start = (bf16[48,96,4,16]{1,3,2,0:T(8,128)(2,1)}, bf16[48,96,4,16]{1,3,2,0:T(8,128)(2,1)S(1)}, u32[]{:S(2)}, u32[]{:S(2)}) collective-permute-start(bf16[48,96,4,16]{1,3,2,0:T(8,128)(2,1)} %get-tuple-element.340), channel_id=1, source_target_pairs={{0,1},{1,2},{2,3},{3,4},{4,5},{5,6},{6,7},{7,0},{8,9},{9,10},{10,1... | collective-permute-start | bytes 1769480 | tf_op jit(solution)/shard_map/while/body/eval_jaxpr/ppermute | solution.py:56
  127.5 21.0 %collective-permute-start.1 = (bf16[48,96,4,16]{1,3,2,0:T(8,128)(2,1)}, bf16[48,96,4,16]{1,3,2,0:T(8,128)(2,1)S(1)}, u32[]{:S(2)}, u32[]{:S(2)}) collective-permute-start(bf16[48,96,4,16]{1,3,2,0:T(8,128)(2,1)} %get-tuple-element.341), channel_id=1, source_target_pairs={{0,1},{1,2},{2,3},{3,4},{4,5},{5,6},{6,7},{7,0},{8,9},{9,10},{10,1... | collective-permute-start | bytes 1769480 | tf_op jit(solution)/shard_map/while/body/eval_jaxpr/ppermute | solution.py:56
  151.1 12.6 %collective-permute-start = (bf16[48,96,4,16]{1,3,2,0:T(8,128)(2,1)}, bf16[48,96,4,16]{1,3,2,0:T(8,128)(2,1)S(1)}, u32[]{:S(2)}, u32[]{:S(2)}) collective-permute-start(bf16[48,96,4,16]{1,3,2,0:T(8,128)(2,1)} %get-tuple-element.340), channel_id=1, source_target_pairs={{0,1},{1,2},{2,3},{3,4},{4,5},{5,6},{6,7},{7,0},{8,9},{9,10},{10,1... | collective-permute-start | bytes 1769480 | tf_op jit(solution)/shard_map/while/body/eval_jaxpr/ppermute | solution.py:56
  151.1 21.0 %collective-permute-start.1 = (bf16[48,96,4,16]{1,3,2,0:T(8,128)(2,1)}, bf16[48,96,4,16]{1,3,2,0:T(8,128)(2,1)S(1)}, u32[]{:S(2)}, u32[]{:S(2)}) collective-permute-start(bf16[48,96,4,16]{1,3,2,0:T(8,128)(2,1)} %get-tuple-element.341), channel_id=1, source_target_pairs={{0,1},{1,2},{2,3},{3,4},{4,5},{5,6},{6,7},{7,0},{8,9},{9,10},{10,1... | collective-permute-start | bytes 1769480 | tf_op jit(solution)/shard_map/while/body/eval_jaxpr/ppermute | solution.py:56
  174.6 12.6 %collective-permute-start = (bf16[48,96,4,16]{1,3,2,0:T(8,128)(2,1)}, bf16[48,96,4,16]{1,3,2,0:T(8,128)(2,1)S(1)}, u32[]{:S(2)}, u32[]{:S(2)}) collective-permute-start(bf16[48,96,4,16]{1,3,2,0:T(8,128)(2,1)} %get-tuple-element.340), channel_id=1, source_target_pairs={{0,1},{1,2},{2,3},{3,4},{4,5},{5,6},{6,7},{7,0},{8,9},{9,10},{10,1... | collective-permute-start | bytes 1769480 | tf_op jit(solution)/shard_map/while/body/eval_jaxpr/ppermute | solution.py:56
  174.7 21.0 %collective-permute-start.1 = (bf16[48,96,4,16]{1,3,2,0:T(8,128)(2,1)}, bf16[48,96,4,16]{1,3,2,0:T(8,128)(2,1)S(1)}, u32[]{:S(2)}, u32[]{:S(2)}) collective-permute-start(bf16[48,96,4,16]{1,3,2,0:T(8,128)(2,1)} %get-tuple-element.341), channel_id=1, source_target_pairs={{0,1},{1,2},{2,3},{3,4},{4,5},{5,6},{6,7},{7,0},{8,9},{9,10},{10,1... | collective-permute-start | bytes 1769480 | tf_op jit(solution)/shard_map/while/body/eval_jaxpr/ppermute | solution.py:56
  198.2 12.6 %collective-permute-start = (bf16[48,96,4,16]{1,3,2,0:T(8,128)(2,1)}, bf16[48,96,4,16]{1,3,2,0:T(8,128)(2,1)S(1)}, u32[]{:S(2)}, u32[]{:S(2)}) collective-permute-start(bf16[48,96,4,16]{1,3,2,0:T(8,128)(2,1)} %get-tuple-element.340), channel_id=1, source_target_pairs={{0,1},{1,2},{2,3},{3,4},{4,5},{5,6},{6,7},{7,0},{8,9},{9,10},{10,1... | collective-permute-start | bytes 1769480 | tf_op jit(solution)/shard_map/while/body/eval_jaxpr/ppermute | solution.py:56
  198.3 21.0 %collective-permute-start.1 = (bf16[48,96,4,16]{1,3,2,0:T(8,128)(2,1)}, bf16[48,96,4,16]{1,3,2,0:T(8,128)(2,1)S(1)}, u32[]{:S(2)}, u32[]{:S(2)}) collective-permute-start(bf16[48,96,4,16]{1,3,2,0:T(8,128)(2,1)} %get-tuple-element.341), channel_id=1, source_target_pairs={{0,1},{1,2},{2,3},{3,4},{4,5},{5,6},{6,7},{7,0},{8,9},{9,10},{10,1... | collective-permute-start | bytes 1769480 | tf_op jit(solution)/shard_map/while/body/eval_jaxpr/ppermute | solution.py:56
  (6 other events, 10.0 us)
where the time goes:
time: 226 us; the launch traced here: 225 us
  waiting for transfers between devices  101 us (45%)
  matrix products  44.4 us (20%)
  other arithmetic  26.3 us (12%)
  blocking collectives  26.1 us (12%)
  local copies, waits for them, and re-layouts  21.2 us (9%)
  starting transfers between devices  5.32 us (2%)
    ppermute x14, waiting for transfers between devices, hop_step(): kv_blocks = lax.ppermute(kv_blocks, 'col', shift_pairs)  92 us
    all_gather x1, blocking collectives, per_device(): bias_cols = lax.all_gather(bias_tile, 'row', axis=0, tiled=True)  26.1 us
    dot_general x8, matrix products, fold_block(): jnp.einsum('ijhd,ikhd->ihjk', queries, key_part, preferred_element_type=j...  25.4 us
    reduce_sum x8, other arithmetic, fold_block(): run_sum = run_sum * rescale + jnp.sum(weights, axis=-1)  21.8 us
    dot_general x8, matrix products, fold_block(): jnp.einsum('ihjk,ikhd->ihjd', weights.astype(jnp.bfloat16), val_part, pre...  13 us
    while x21, local copies, waits for them, and re-layouts  12.4 us
    all_to_all x1, waiting for transfers between devices, per_device(): bias_rows = lax.all_to_all(bias_cols, 'col', 0, 1, tiled=True)  9.19 us
    dynamic_slice x8, local copies, waits for them, and re-layouts, fold_block(): lax.dynamic_slice_in_dim(full_bias, src_col * col_len, col_len, axis=2)  6.66 us
  transfers between devices with their start and end apart: 15, of which 15 were waited for; matrix products, arithmetic and copies ran while one was open for 26% of the time, Pallas kernels for 0%

commit v1 on v0

v1 whole, which is shorter than its diff:
```python
import functools

import jax
import jax.numpy as jnp
from jax import lax
from jax.experimental import pallas as pl
from jax.experimental.pallas import tpu as pltpu
from jax.sharding import PartitionSpec as P

LN_EPS = 1e-5
NEG = -1e9
MESH = pl.DeviceIdType.MESH
F32 = jnp.float32
BF16 = jnp.bfloat16

PAIRS, COLS, CH = 24, 96, 64
HEADS, HEAD = 4, 16
KEYS = 768
BLOCKS = 8


def dot(a, b, ca=1, cb=0):
    return lax.dot_general(a, b, (((ca,), (cb,)), ((), ())), preferred_element_type=F32)


def iota(shape, dim):
    return lax.broadcasted_iota(jnp.int32, shape, dim)


def column(row_ref, n):
    eye = iota((n, n), 0) == iota((n, n), 1)
    return jnp.sum(jnp.where(eye, jnp.broadcast_to(row_ref[...], (n, n)), 0.0), axis=1, keepdims=True)


def block_diag(w):
    zero = jnp.zeros_like(w)
    return jnp.concatenate(
        [jnp.concatenate([w, zero], axis=1), jnp.concatenate([zero, w], axis=1)], axis=0
    )


def norm_kernel(z_ref, gamma_ref, beta_ref, wbt_ref, a_ref, b_ref, bias_acc):
    gamma = column(gamma_ref, CH)
    beta = column(beta_ref, CH)
    pick = (iota((192, HEADS), 0) // 48 == iota((192, HEADS), 1)).astype(F32).astype(BF16)
    per_head = dot(pick, wbt_ref[...]).astype(BF16)
    wide = jnp.concatenate([per_head, per_head], axis=1)
    keep = iota((192, 128), 0) % 2 == iota((192, 128), 1) // CH
    wide = jnp.where(keep, wide.astype(F32), 0.0).astype(BF16)
    lane_pair = (iota((COLS, 192), 1) % 48) // 2

    def body(p, carry):
        halves = []
        for half in range(2):
            x = z_ref[2 * p + half].astype(F32)
            mean = jnp.sum(x, axis=0, keepdims=True) * (1.0 / CH)
            centered = x - mean
            var = jnp.sum(centered * centered, axis=0, keepdims=True) * (1.0 / CH)
            halves.append(centered * lax.rsqrt(var + LN_EPS) * gamma + beta)
        a_t = jnp.concatenate(halves, axis=0)
        a = jnp.transpose(a_t).astype(BF16)
        a_ref[p] = a
        bias = dot(a, wide, 1, 1)
        bias_acc[...] = jnp.where(lane_pair == p, bias, bias_acc[...])
        return carry

    lax.fori_loop(0, PAIRS, body, 0)
    bias = bias_acc[...]
    b_ref[0:96, :] = bias[:, 0:128].astype(BF16)
    tail = jnp.concatenate([bias[0:48, 128:192], bias[48:96, 128:192]], axis=1)
    b_ref[96:144, :] = tail.astype(BF16)


def norm_call(z_t, gamma, beta, wb_t):
    return pl.pallas_call(
        norm_kernel,
        out_shape=(
            jax.ShapeDtypeStruct((PAIRS, COLS, 2 * CH), BF16),
            jax.ShapeDtypeStruct((144, 128), BF16),
        ),
        in_specs=[pl.BlockSpec(memory_space=pltpu.VMEM)] * 4,
        out_specs=(pl.BlockSpec(memory_space=pltpu.VMEM),) * 2,
        scratch_shapes=[pltpu.VMEM((COLS, 192), F32)],
        cost_estimate=pl.CostEstimate(flops=10**8, bytes_accessed=2 * 10**6, transcendentals=4608),
        name="norm",
    )(z_t, gamma, beta, wb_t)


def exchange_kernel(
    a_ref, b_ref, all_a, all_b,
    send_b1, recv_b1, send_b2, recv_b2, send_a, recv_a, send_f, recv_f,
):
    row = lax.axis_index("row")
    col = lax.axis_index("col")
    z, y = row // 4, row % 4
    x, core = col // 2, col % 2
    half = PAIRS // 2

    right = {"row": row, "col": ((x + 1) % 4) * 2 + core}
    left = {"row": row, "col": ((x + 3) % 4) * 2 + core}
    partner = {"row": row, "col": x * 2 + (1 - core)}
    swap_row, swap_col = 4 * x + y, 2 * z + y // 2
    is_relay = core == y // 2
    swap_self = jnp.logical_and(z == x, is_relay)

    barrier = pltpu.get_barrier_semaphore()

    def hello(dev):
        pl.semaphore_signal(barrier, inc=1, device_id=dev, device_id_type=MESH)

    for step in range(1, 16):
        hello({"row": (row + step) % 16, "col": col})
    hello(right)
    hello(left)
    hello(partner)

    @pl.when(jnp.logical_not(swap_self))
    def _():
        hello({"row": swap_row, "col": swap_col})

    for c in range(2):
        @pl.when(jnp.logical_and(is_relay, jnp.logical_not(jnp.logical_and(z == x, core == c))))
        def _():
            hello({"row": 4 * x + y, "col": 2 * z + c})

    from_dest = jnp.where(swap_self, 0, 1)
    from_sources = jnp.where(is_relay, jnp.where(z == x, 1, 2), 0)
    pl.semaphore_wait(barrier, 18 + from_dest + from_sources)

    def bias1(c):
        return pltpu.make_async_remote_copy(
            src_ref=b_ref,
            dst_ref=all_b.at[y % 2, 2 * x + c],
            send_sem=send_b1,
            recv_sem=recv_b1.at[c],
            device_id={"row": swap_row, "col": swap_col},
            device_id_type=MESH,
        )

    for c in range(2):
        @pl.when(jnp.logical_and(core == c, jnp.logical_not(swap_self)))
        def _():
            bias1(c).start()

    @pl.when(swap_self)
    def _():
        all_b[y % 2, col] = b_ref[...]

    def slot(ref, hf, c):
        return ref.at[pl.ds(hf * half, half), pl.ds(pl.multiple_of(c * COLS, COLS), COLS)]

    def a_copy(src, hf, c, sem, dev):
        return pltpu.make_async_remote_copy(
            src_ref=src, dst_ref=slot(all_a, hf, c),
            send_sem=send_a.at[sem], recv_sem=recv_a.at[sem],
            device_id=dev, device_id_type=MESH,
        )

    def own(hf):
        return a_ref.at[pl.ds(hf * half, half)]

    a_copy(own(0), 0, col, 0, right).start()
    a_copy(own(1), 1, col, 3, left).start()
    a_copy(own(1), 1, col, 1, right).start()
    a_copy(own(0), 0, col, 2, left).start()

    def f_copy(src, hf, c, sem):
        return pltpu.make_async_remote_copy(
            src_ref=src, dst_ref=slot(all_a, hf, c),
            send_sem=send_f.at[sem], recv_sem=recv_f.at[sem],
            device_id=partner, device_id_type=MESH,
        )

    for hf in range(2):
        f_copy(own(hf), hf, col, 6 + hf).start()
    all_a[:, pl.ds(pl.multiple_of(col * COLS, COLS), COLS), :] = a_ref[...]

    par = y % 2

    def bias2(step, src_row):
        sz, sy = src_row // 4, src_row % 4
        ref = all_b.at[sy % 2, pl.ds(2 * sz, 2)]
        return pltpu.make_async_remote_copy(
            src_ref=ref, dst_ref=ref,
            send_sem=send_b2.at[step], recv_sem=recv_b2.at[sy % 2, sz],
            device_id={"row": (row + step) % 16, "col": col}, device_id_type=MESH,
        )

    @pl.when(is_relay)
    def _():
        for c in range(2):
            @pl.when(jnp.logical_not(jnp.logical_and(z == x, core == c)))
            def _():
                pltpu.make_async_remote_copy(
                    src_ref=b_ref, dst_ref=all_b.at[par, 2 * z + c],
                    send_sem=send_b1, recv_sem=recv_b1.at[c],
                    device_id={"row": swap_row, "col": swap_col}, device_id_type=MESH,
                ).wait_recv()
        for step in range(1, 16):
            bias2(step, row).start()

    cl, cr, co = ((x + 3) % 4) * 2 + core, ((x + 1) % 4) * 2 + core, ((x + 2) % 4) * 2 + core

    def arrived(hf, c, sem):
        a_copy(slot(all_a, hf, c), hf, c, sem, right).wait_recv()

    arrived(0, cl, 0)
    a_copy(slot(all_a, 0, cl), 0, cl, 4, right).start()
    f_copy(slot(all_a, 0, cl), 0, cl, 0).start()
    arrived(1, cr, 3)
    a_copy(slot(all_a, 1, cr), 1, cr, 5, left).start()
    f_copy(slot(all_a, 1, cr), 1, cr, 3).start()
    arrived(1, cl, 1)
    f_copy(slot(all_a, 1, cl), 1, cl, 1).start()
    arrived(0, cr, 2)
    f_copy(slot(all_a, 0, cr), 0, cr, 2).start()
    arrived(0, co, 4)
    f_copy(slot(all_a, 0, co), 0, co, 4).start()
    arrived(1, co, 5)
    f_copy(slot(all_a, 1, co), 1, co, 5).start()

    for sy in range(2):
        for sz in range(4):
            @pl.when(jnp.logical_not(row == sz * 4 + 2 * core + sy))
            def _():
                ref = all_b.at[sy, pl.ds(2 * sz, 2)]
                pltpu.make_async_remote_copy(
                    src_ref=ref, dst_ref=ref, send_sem=send_b2.at[1], recv_sem=recv_b2.at[sy, sz],
                    device_id=partner, device_id_type=MESH,
                ).wait_recv()

    def from_partner(hf, c, sem):
        f_copy(slot(all_a, hf, c), hf, c, sem).wait_recv()

    other = 1 - core
    pl_, pr_, po_ = ((x + 3) % 4) * 2 + other, ((x + 1) % 4) * 2 + other, ((x + 2) % 4) * 2 + other
    from_partner(0, 2 * x + other, 6)
    from_partner(1, 2 * x + other, 7)
    from_partner(0, pl_, 0)
    from_partner(1, pr_, 3)
    from_partner(1, pl_, 1)
    from_partner(0, pr_, 2)
    from_partner(0, po_, 4)
    from_partner(1, po_, 5)

    for c in range(2):
        @pl.when(jnp.logical_and(core == c, jnp.logical_not(swap_self)))
        def _():
            bias1(c).wait_send()

    @pl.when(is_relay)
    def _():
        for step in range(1, 16):
            bias2(step, row).wait_send()

    for sem in range(6):
        a_copy(own(0), 0, col, sem, right).wait_send()
    for sem in range(8):
        f_copy(own(0), 0, col, sem).wait_send()


def exchange_call(a, b):
    dma = pltpu.SemaphoreType.DMA
    return pl.pallas_call(
        exchange_kernel,
        out_shape=(
            jax.ShapeDtypeStruct((PAIRS, KEYS, 2 * CH), BF16),
            jax.ShapeDtypeStruct((2, 8, 144, 128), BF16),
        ),
        in_specs=[pl.BlockSpec(memory_space=pltpu.VMEM)] * 2,
        out_specs=(pl.BlockSpec(memory_space=pltpu.VMEM),) * 2,
        scratch_shapes=[
            dma(()), dma((2,)), dma((16,)), dma((2, 4)), dma((6,)), dma((6,)), dma((8,)), dma((8,)),
        ],
        compiler_params=pltpu.CompilerParams(collective_id=0, has_side_effects=True),
        cost_estimate=pl.CostEstimate(flops=10**9, bytes_accessed=5 * 10**6, transcendentals=0),
        name="exchange",
    )(a, b)


TILE_ROWS = ((0, 48), (32, 96), (80, 128))


def attention_kernel(
    a_ref, own_ref, z_ref, b_ref, mask_ref, gamma_ref, beta_ref, wb_ref,
    wq_ref, wk_ref, wv_ref, wg_ref, wo_ref, a_hbm,
    out_ref,
    bias_s, w_s, kk_s, vt_s, qm_s, p_s, l_s, bad_s, nk_s, a_s, dma_sem,
):
    pid = pl.program_id(0)

    @pl.when(pid == 0)
    def _():
        length = jnp.sum((mask_ref[...] > 0).astype(F32)).astype(jnp.int32)
        def top(ref):
            return jnp.max(jnp.abs(ref[...].astype(F32)))

        norm_max = 8.1 * top(gamma_ref) + 1.1 * top(beta_ref)
        q_max = CH * norm_max * top(wq_ref)
        k_max = CH * norm_max * top(wk_ref)
        limit = 4.2 * q_max * k_max + 1.1 * CH * norm_max * top(wb_ref)
        nk_s[0] = jnp.where(limit < 2e8, (length + 127) // 128, 6)
        bad_s[...] = jnp.zeros_like(bad_s)
        w_s[0] = block_diag(wk_ref[...])
        w_s[1] = jnp.transpose(block_diag(wv_ref[...]).astype(F32)).astype(BF16)
        w_s[2] = block_diag(wq_ref[...])
        w_s[3] = jnp.transpose(block_diag(wg_ref[...]).astype(F32)).astype(BF16)
        w_s[4] = jnp.transpose(block_diag(wo_ref[...]).astype(F32)).astype(BF16)
        for c in range(8):
            tiles = []
            for par in range(2):
                t = b_ref[par, c].astype(F32)
                tail = t[96:144]
                tiles.append(jnp.concatenate(
                    [t[0:96], jnp.concatenate([tail[:, 0:64], tail[:, 64:128]], axis=0)], axis=1))
            full = jnp.concatenate(
                [tiles[par][:, 48 * h:48 * h + 48] for h in range(HEADS) for par in range(2)], axis=1)
            key = iota((COLS, 384), 0) + c * COLS
            bias_s[c * COLS:(c + 1) * COLS, :] = full + jnp.where(key < length, 0.0, NEG)

    def project(a, a_own):
        kk_s[...] = dot(a, w_s[0]).astype(BF16)
        vt_s[...] = dot(w_s[1], a, 1, 1).astype(BF16)
        q = (dot(a_own, w_s[2]) * HEAD ** -0.5)
        block = iota((COLS, 128), 1) // HEAD
        for b in range(BLOCKS):
            qm_s[b * COLS:(b + 1) * COLS, :] = jnp.where(block == b, q, 0.0).astype(BF16)
        return jax.nn.sigmoid(dot(w_s[3], a_own, 1, 1))

    def bias_of(t, k0, nk):
        lo = (2 * t) % 3
        if lo < 2:
            return bias_s[k0:k0 + nk, lo * 128:lo * 128 + 256]
        return jnp.concatenate([bias_s[k0:k0 + nk, 256:384], bias_s[k0:k0 + nk, 0:128]], axis=1)

    def finish(p, gate, o_tiles):
        parts = []
        for b in range(BLOCKS):
            pieces = []
            for t in range(3):
                lo, hi = max(b * 96, t * 256), min(b * 96 + 96, t * 256 + 256)
                if lo < hi:
                    r = b * HEAD - TILE_ROWS[t][0]
                    pieces.append(o_tiles[t][r:r + HEAD, lo - t * 256:hi - t * 256])
            parts.append(pieces[0] if len(pieces) == 1 else jnp.concatenate(pieces, axis=1))
        o = jnp.concatenate(parts, axis=0)
        gated = (gate * o).astype(BF16)
        update = dot(w_s[4], gated)
        for hf in range(2):
            res = z_ref[2 * p + hf].astype(F32) + update[hf * CH:(hf + 1) * CH]
            out_ref[2 * p + hf] = res.astype(BF16)

    def fast(p, n_chunks):
        nk = n_chunks * 128
        gate = project(a_ref[0], own_ref[p])
        outs = []
        for t in range(3):
            lanes = slice(t * 256, t * 256 + 256)
            qm = qm_s[lanes, :]
            total = jnp.zeros((8, 256), F32)
            for kc in range(n_chunks):
                keys = slice(kc * 128, kc * 128 + 128)
                e = jnp.exp(dot(kk_s[keys, :], qm, 1, 1) + bias_of(t, kc * 128, 128))
                total = total + jnp.sum(e.reshape(16, 8, 256), axis=0)
                p_s[keys, lanes] = e.astype(BF16)
            r0, r1 = TILE_ROWS[t]
            o = dot(vt_s[r0:r1, 0:nk], p_s[0:nk, lanes])
            total = jnp.sum(total, axis=0, keepdims=True)
            o_max = jnp.max(jnp.abs(o), axis=0, keepdims=True)
            good = (total > 1e-12) & (total < 1e25) & (o_max < 1e35)
            bad_s[0:1, lanes] = jnp.maximum(bad_s[0:1, lanes], jnp.where(good, 0.0, 1.0))
            outs.append(o * (1.0 / total))
        finish(p, gate, outs)

    for n_chunks in range(2, 7):
        @pl.when(nk_s[0] == n_chunks)
        def _():
            fast(pid, n_chunks)

    @pl.when(pid == PAIRS - 1)
    def _():
        @pl.when(jnp.max(bad_s[...]) > 0.0)
        def _():
            def body(p, carry):
                cp = pltpu.make_async_copy(a_hbm.at[p], a_s, dma_sem)
                cp.start()
                cp.wait()
                gate = project(a_s[...], own_ref[p])
                outs = []
                for t in range(3):
                    lanes = slice(t * 256, t * 256 + 256)
                    qm = qm_s[lanes, :]
                    top = jnp.full((1, 256), -jnp.inf, F32)
                    for kc in range(6):
                        keys = slice(kc * 128, kc * 128 + 128)
                        s = dot(kk_s[keys, :], qm, 1, 1) + bias_of(t, kc * 128, 128)
                        l_s[keys, :] = s
                        top = jnp.maximum(top, jnp.max(s, axis=0, keepdims=True))
                    total = jnp.zeros((1, 256), F32)
                    for kc in range(6):
                        keys = slice(kc * 128, kc * 128 + 128)
                        e = jnp.exp(l_s[keys, :] - top)
                        total = total + jnp.sum(e, axis=0, keepdims=True)
                        p_s[keys, lanes] = e.astype(BF16)
                    r0, r1 = TILE_ROWS[t]
                    outs.append(dot(vt_s[r0:r1, :], p_s[:, lanes]) * (1.0 / total))
                finish(p, gate, outs)
                return carry

            lax.fori_loop(0, PAIRS, body, 0)


def attention_call(all_a, a, z_t, all_b, mask, gamma, beta, wb_t, wq, wk, wv, wg, wo):
    pairs = all_a.shape[0]

    def whole(arr):
        nd = arr.ndim
        return pl.BlockSpec(arr.shape, lambda i: (0,) * nd)

    small = (a, z_t, all_b, mask, gamma, beta, wb_t, wq, wk, wv, wg, wo)
    return pl.pallas_call(
        attention_kernel,
        grid=(pairs,),
        out_shape=jax.ShapeDtypeStruct(z_t.shape, BF16),
        in_specs=[pl.BlockSpec((1, KEYS, 2 * CH), lambda i: (i, 0, 0))]
        + [whole(s) for s in small]
        + [pl.BlockSpec(memory_space=pl.ANY)],
        out_specs=whole(z_t),
        scratch_shapes=[
            pltpu.VMEM((KEYS, 384), F32),
            pltpu.VMEM((5, 128, 128), BF16),
            pltpu.VMEM((KEYS, 128), BF16),
            pltpu.VMEM((128, KEYS), BF16),
            pltpu.VMEM((KEYS, 128), BF16),
            pltpu.VMEM((KEYS, KEYS), BF16),
            pltpu.VMEM((KEYS, 256), F32),
            pltpu.VMEM((8, KEYS), F32),
            pltpu.SMEM((1,), jnp.int32),
            pltpu.VMEM((KEYS, 128), BF16),
            pltpu.SemaphoreType.DMA(()),
        ],
        compiler_params=pltpu.CompilerParams(dimension_semantics=("arbitrary",)),
        cost_estimate=pl.CostEstimate(flops=10**10, bytes_accessed=8 * 10**6, transcendentals=14 * 10**6),
        name="attention",
    )(all_a, *small, all_a)


def solution(mesh):
    tile_spec = P(("dp", "row"), "col", None)

    def per_device(pair_tile, res_mask, ln_gamma, ln_beta, w_q, w_k, w_v, w_b, w_g, w_o):
        z_t = jnp.transpose(pair_tile, (0, 2, 1))
        gamma = ln_gamma.reshape(1, CH)
        beta = ln_beta.reshape(1, CH)
        wb_t = jnp.transpose(w_b)
        a, b = norm_call(z_t, gamma, beta, wb_t)
        all_a, all_b = exchange_call(a, b)
        out_t = attention_call(
            all_a, a, z_t, all_b, res_mask.reshape(6, 128), gamma, beta, wb_t, w_q, w_k, w_v, w_g, w_o
        )
        return jnp.transpose(out_t, (0, 2, 1))

    return jax.shard_map(
        per_device, mesh=mesh,
        in_specs=(tile_spec, P("dp"), P(), P(), P(), P(), P(), P(), P(), P()),
        out_specs=tile_spec, check_vma=False,
    )
```

time: 226 us -> 82.7 us (0.37)
  the two profiles are of different devices: /device:TPU:0 before, /device:TPU:1 now
where the time goes in v1:
time: 82.7 us; the launch traced here: 82.5 us
  Pallas kernels  82.5 us (100%)
    pallas_call x1, Pallas kernels, exchange_call(): pl.pallas_call(exchange_kernel, out_shape=(jax.ShapeDtypeStruct((PAIRS, K...  37.2 us
    pallas_call x1, Pallas kernels, attention_call(): pl.pallas_call(attention_kernel, grid=(pairs,), out_shape=jax.ShapeDtypeS...  37.1 us
    pallas_call x1, Pallas kernels, norm_call(): pl.pallas_call(norm_kernel, out_shape=(jax.ShapeDtypeStruct((PAIRS, COLS,...  8.24 us

profile of v1, /device:TPU:1, one launch (start us, length us, event | category | flops | bytes accessed | tf_op | source)
XLA Modules:
  0.0 82.5 jit_solution(14143638339331501657)
XLA Ops:
  0.0 8.2 %norm.1 = (bf16[24,96,128]{2,1,0:T(8,128)(2,1)}, bf16[144,128]{1,0:T(8,128)(2,1)}) custom-call(bf16[48,64,96]{2,1,0:T(8,128)(2,1)} %bitcast.6, f32[1,64]{1,0:T(1,128)} %bitcast.10, f32[1,64]{1,0:T(1,128)} %bitcast.12, bf16[4,64]{1,0:T(4,128)(2,1)} %bitcast.8), custom_call_target="tpu_custom_call" | custom-call | flops 100000000 | bytes 2000000 | tf_op jit(solution)/shard_map/norm/pallas_call | solution.py:75
  8.2 37.2 %exchange.1 = (bf16[24,768,128]{2,1,0:T(8,128)(2,1)}, bf16[2,8,144,128]{3,2,1,0:T(8,128)(2,1)}) custom-call(bf16[24,96,128]{2,1,0:T(8,128)(2,1)} %get-tuple-element.9.a_ref.own_ref, bf16[144,128]{1,0:T(8,128)(2,1)} %get-tuple-element.10.b_ref), custom_call_target="tpu_custom_call" | custom-call | flops 1000000000 | bytes 5000000 | tf_op jit(solution)/shard_map/exchange/pallas_call | solution.py:264
  45.5 37.1 %attention.1 = bf16[48,64,96]{2,1,0:T(8,128)(2,1)} custom-call(bf16[24,768,128]{2,1,0:T(8,128)(2,1)} %get-tuple-element.11.a_ref.a_hbm, bf16[24,96,128]{2,1,0:T(8,128)(2,1)} %get-tuple-element.9.a_ref.own_ref, bf16[48,64,96]{2,1,0:T(8,128)(2,1)} %bitcast.7, bf16[2,8,144,128]{3,2,1,0:T(8,128)(2,1)} %get-tuple-element.12.b_ref, s32[6,128]{1,0:T(8,128)} %bitcast.14, ...), custom_call_target="tpu_custom_call" | custom-call | flops 10000000000 | bytes 8000000 | tf_op jit(solution)/shard_map/attention/pallas_call | solution.py:421

commit v2 on v0

v2 whole, which is shorter than its diff:
```python
import functools

import jax
import jax.numpy as jnp
from jax import lax
from jax.experimental import pallas as pl
from jax.experimental.pallas import tpu as pltpu
from jax.sharding import PartitionSpec as P

LN_EPS = 1e-5
NEG = -1e9
MESH = pl.DeviceIdType.MESH
F32 = jnp.float32
BF16 = jnp.bfloat16

PAIRS, COLS, CH = 24, 96, 64
HEADS, HEAD = 4, 16
KEYS = 768
BLOCKS = 8
GROUPS, GP = 6, 4
LIVE = 672
CHUNK = 112
TILE_ROWS = ((0, 48), (32, 96), (80, 128))


def dot(a, b, ca=1, cb=0):
    return lax.dot_general(a, b, (((ca,), (cb,)), ((), ())), preferred_element_type=F32)


def iota(shape, dim):
    return lax.broadcasted_iota(jnp.int32, shape, dim)


def column(row_ref, n):
    eye = iota((n, n), 0) == iota((n, n), 1)
    return jnp.sum(jnp.where(eye, jnp.broadcast_to(row_ref[...], (n, n)), 0.0), axis=1, keepdims=True)


def block_diag(w):
    zero = jnp.zeros_like(w)
    return jnp.concatenate(
        [jnp.concatenate([w, zero], axis=1), jnp.concatenate([zero, w], axis=1)], axis=0
    )


def load(pairs, sems):
    copies = [pltpu.make_async_copy(src, dst, sems.at[i]) for i, (src, dst) in enumerate(pairs)]
    for copy in copies:
        copy.start()
    return copies


def fill_weights(w_s, wq_ref, wk_ref, wv_ref, wg_ref, wo_ref):
    w_s[0] = block_diag(wq_ref[...])
    w_s[1] = jnp.transpose(block_diag(wg_ref[...]).astype(F32)).astype(BF16)
    w_s[2] = jnp.transpose(block_diag(wo_ref[...]).astype(F32)).astype(BF16)
    w_s[3] = block_diag(wk_ref[...])
    w_s[4] = jnp.transpose(block_diag(wv_ref[...]).astype(F32)).astype(BF16)


def fill_bias(bias_s, all_b, mask_ref):
    length = jnp.sum((mask_ref[...] > 0).astype(F32), axis=1, keepdims=True)
    length = jnp.sum(length, axis=0, keepdims=True)
    for c in range(8):
        tiles = []
        for par in range(2):
            t = all_b[par, c].astype(F32)
            tail = t[96:144]
            tiles.append(jnp.concatenate(
                [t[0:96], jnp.concatenate([tail[:, 0:64], tail[:, 64:128]], axis=0)], axis=1))
        full = jnp.concatenate(
            [tiles[par][:, 48 * h:48 * h + 48] for h in range(HEADS) for par in range(2)], axis=1)
        key = (iota((COLS, 384), 0) + c * COLS).astype(F32)
        bias_s[c * COLS:(c + 1) * COLS, :] = full + jnp.where(key < length, 0.0, NEG)


def bias_of(bias_s, t, k0, nk):
    lo = (2 * t) % 3
    if lo < 2:
        return bias_s[k0:k0 + nk, lo * 128:lo * 128 + 256]
    return jnp.concatenate([bias_s[k0:k0 + nk, 256:384], bias_s[k0:k0 + nk, 0:128]], axis=1)


def fill_queries(qm, own, wq):
    q = dot(own, wq) * HEAD ** -0.5
    block = iota((COLS, 128), 1) // HEAD
    for b in range(BLOCKS):
        qm[b * COLS:(b + 1) * COLS, :] = jnp.where(block == b, q, 0.0).astype(BF16)


def assemble(o_tiles):
    parts = []
    for b in range(BLOCKS):
        pieces = []
        for t in range(3):
            lo, hi = max(b * 96, t * 256), min(b * 96 + 96, t * 256 + 256)
            if lo < hi:
                r = b * HEAD - TILE_ROWS[t][0]
                pieces.append(o_tiles[t][r:r + HEAD, lo - t * 256:hi - t * 256])
        parts.append(pieces[0] if len(pieces) == 1 else jnp.concatenate(pieces, axis=1))
    return jnp.concatenate(parts, axis=0)


def write_rows(p, own, o, w_s, z_ref, out_ref):
    gate = jax.nn.sigmoid(dot(w_s[1], own, 1, 1))
    update = dot(w_s[2], (gate * o).astype(BF16))
    for hf in range(2):
        res = z_ref[2 * p + hf].astype(F32) + update[hf * CH:(hf + 1) * CH]
        out_ref[2 * p + hf] = res.astype(BF16)


def fused_kernel(
    z_hbm, gamma_hbm, beta_hbm, wb_hbm, mask_hbm, wq_hbm, wk_hbm, wv_hbm, wg_hbm, wo_hbm,
    out_hbm, all_a_hbm, all_b_hbm, bad_hbm,
    z_ref, gamma_ref, beta_ref, wb_ref, mask_ref, wq_ref, wk_ref, wv_ref, wg_ref, wo_ref, in_sems,
    own_a, own_b, all_a, all_b, out_ref, bias_acc, bias_s, w_s,
    kk0, kk1, vt0, vt1, qm0, qm1, p0, p1, sum0, sum1, o0, o1, bad_s,
    send_b1, recv_b1, send_b2, recv_b2, send_d, recv_d, send_r, recv_r, send_f, recv_f, out_sems,
):
    kk_s, vt_s, qm_s, p_s, sum_s, o_s = (kk0, kk1), (vt0, vt1), (qm0, qm1), (p0, p1), (sum0, sum1), (o0, o1)
    row = lax.axis_index("row")
    col = lax.axis_index("col")
    z, y = row // 4, row % 4
    x, core = col // 2, col % 2

    copies = load(
        [(gamma_hbm, gamma_ref), (beta_hbm, beta_ref), (wb_hbm, wb_ref)]
        + [(z_hbm.at[pl.ds(12 * n, 12)], z_ref.at[pl.ds(12 * n, 12)]) for n in range(4)]
        + [(mask_hbm, mask_ref), (wq_hbm, wq_ref), (wk_hbm, wk_ref), (wv_hbm, wv_ref), (wg_hbm, wg_ref),
           (wo_hbm, wo_ref)], in_sems)

    right = {"row": row, "col": ((x + 1) % 4) * 2 + core}
    left = {"row": row, "col": ((x + 3) % 4) * 2 + core}
    partner = {"row": row, "col": x * 2 + (1 - core)}
    swap = {"row": 4 * x + y, "col": 2 * z + y // 2}
    is_relay = core == y // 2
    swap_self = jnp.logical_and(z == x, is_relay)

    barrier = pltpu.get_barrier_semaphore()

    def hello(dev):
        pl.semaphore_signal(barrier, inc=1, device_id=dev, device_id_type=MESH)

    for step in range(1, 16):
        hello({"row": (row + step) % 16, "col": col})
    hello(right)
    hello(left)
    hello(partner)

    @pl.when(jnp.logical_not(swap_self))
    def _():
        hello(swap)

    for c in range(2):
        @pl.when(jnp.logical_and(is_relay, jnp.logical_not(jnp.logical_and(z == x, core == c))))
        def _():
            hello({"row": 4 * x + y, "col": 2 * z + c})

    for copy in copies[:3]:
        copy.wait()
    gamma = column(gamma_ref, CH)
    beta = column(beta_ref, CH)
    pick = (iota((192, HEADS), 0) // 48 == iota((192, HEADS), 1)).astype(F32).astype(BF16)
    per_head = dot(pick, wb_ref[...]).astype(BF16)
    wide = jnp.concatenate([per_head, per_head], axis=1)
    keep = iota((192, 128), 0) % 2 == iota((192, 128), 1) // CH
    wide = jnp.where(keep, wide.astype(F32), 0.0).astype(BF16)
    lane_pair = (iota((COLS, 192), 1) % 48) // 2

    def norm_pair(p, carry):
        halves = []
        for half in range(2):
            v = z_ref[2 * p + half].astype(F32)
            mean = jnp.sum(v, axis=0, keepdims=True) * (1.0 / CH)
            centered = v - mean
            var = jnp.sum(centered * centered, axis=0, keepdims=True) * (1.0 / CH)
            halves.append(centered * lax.rsqrt(var + LN_EPS) * gamma + beta)
        a = jnp.transpose(jnp.concatenate(halves, axis=0)).astype(BF16)
        own_a[p] = a
        bias_acc[...] = jnp.where(lane_pair == p, dot(a, wide, 1, 1), bias_acc[...])
        return carry

    for n in range(4):
        copies[3 + n].wait()
        lax.fori_loop(6 * n, 6 * n + 6, norm_pair, 0, unroll=6)
    bias = bias_acc[...]
    own_b[0:96, :] = bias[:, 0:128].astype(BF16)
    own_b[96:144, :] = jnp.concatenate([bias[0:48, 128:192], bias[48:96, 128:192]], axis=1).astype(BF16)

    from_dest = jnp.where(swap_self, 0, 1)
    from_sources = jnp.where(is_relay, jnp.where(z == x, 1, 2), 0)
    pl.semaphore_wait(barrier, 18 + from_dest + from_sources)

    def bias1(c):
        return pltpu.make_async_remote_copy(
            src_ref=own_b, dst_ref=all_b.at[y % 2, 2 * x + c], send_sem=send_b1, recv_sem=recv_b1.at[c],
            device_id=swap, device_id_type=MESH,
        )

    for c in range(2):
        @pl.when(jnp.logical_and(core == c, jnp.logical_not(swap_self)))
        def _():
            bias1(c).start()

    def slot(g, c):
        return all_a.at[pl.ds(g * GP, GP), pl.ds(pl.multiple_of(c * COLS, COLS), COLS)]

    def own(g):
        return own_a.at[pl.ds(g * GP, GP)]

    def direct(src, g, c, way):
        return pltpu.make_async_remote_copy(
            src_ref=src, dst_ref=slot(g, c), send_sem=send_d.at[way, g], recv_sem=recv_d.at[way, g],
            device_id=left if way else right, device_id_type=MESH,
        )

    def relay(g, c, way):
        return pltpu.make_async_remote_copy(
            src_ref=slot(g, c), dst_ref=slot(g, c), send_sem=send_r.at[g], recv_sem=recv_r.at[g],
            device_id=left if way else right, device_id_type=MESH,
        )

    def forward(src, g, c, kind):
        return pltpu.make_async_remote_copy(
            src_ref=src, dst_ref=slot(g, c), send_sem=send_f.at[kind, g], recv_sem=recv_f.at[kind, g],
            device_id=partner, device_id_type=MESH,
        )

    for g in range(GROUPS):
        direct(own(g), g, col, 0).start()
        direct(own(g), g, col, 1).start()
        forward(own(g), g, col, 0).start()

    @pl.when(swap_self)
    def _():
        all_b[y % 2, col] = own_b[...]

    all_a[:, pl.ds(pl.multiple_of(col * COLS, COLS), COLS), :] = own_a[...]
    for copy in copies[7:]:
        copy.wait()
    fill_weights(w_s, wq_ref, wk_ref, wv_ref, wg_ref, wo_ref)

    def peak(ref):
        return jnp.max(jnp.max(jnp.abs(ref[...].astype(F32)), axis=1, keepdims=True), axis=0, keepdims=True)

    norm_max = 8.1 * peak(gamma_ref) + 1.1 * peak(beta_ref)
    limit = 4.2 * (CH * norm_max * peak(wq_ref)) * (CH * norm_max * peak(wk_ref)) + 1.1 * CH * norm_max * peak(wb_ref)
    bad_s[...] = jnp.broadcast_to(jnp.where(limit < 2e8, 0.0, 1.0), bad_s.shape)

    def bias2(step, src_row):
        sz, sy = src_row // 4, src_row % 4
        ref = all_b.at[sy % 2, pl.ds(2 * sz, 2)]
        return pltpu.make_async_remote_copy(
            src_ref=ref, dst_ref=ref, send_sem=send_b2.at[step], recv_sem=recv_b2.at[sy % 2, sz],
            device_id={"row": (row + step) % 16, "col": col}, device_id_type=MESH,
        )

    @pl.when(is_relay)
    def _():
        for c in range(2):
            @pl.when(jnp.logical_not(jnp.logical_and(z == x, core == c)))
            def _():
                pltpu.make_async_remote_copy(
                    src_ref=own_b, dst_ref=all_b.at[y % 2, 2 * z + c], send_sem=send_b1, recv_sem=recv_b1.at[c],
                    device_id=swap, device_id_type=MESH,
                ).wait_recv()
        for step in range(1, 16):
            bias2(step, row).start()

    cl, cr, co = ((x + 3) % 4) * 2 + core, ((x + 1) % 4) * 2 + core, ((x + 2) % 4) * 2 + core
    for g in range(GROUPS):
        direct(slot(g, cl), g, cl, 0).wait_recv()
        if g % 2 == 0:
            relay(g, cl, 0).start()
        forward(slot(g, cl), g, cl, 1).start()
        direct(slot(g, cr), g, cr, 1).wait_recv()
        if g % 2 == 1:
            relay(g, cr, 1).start()
        forward(slot(g, cr), g, cr, 2).start()

    for sy in range(2):
        for sz in range(4):
            @pl.when(jnp.logical_not(row == sz * 4 + 2 * core + sy))
            def _():
                ref = all_b.at[sy, pl.ds(2 * sz, 2)]
                pltpu.make_async_remote_copy(
                    src_ref=ref, dst_ref=ref, send_sem=send_b2.at[1], recv_sem=recv_b2.at[sy, sz],
                    device_id=partner, device_id_type=MESH,
                ).wait_recv()
    fill_bias(bias_s, all_b, mask_ref)
    b_out = pltpu.make_async_copy(all_b, all_b_hbm, out_sems.at[0])
    b_out.start()

    def relayed(g):
        relay(g, co, 0).wait_recv()
        forward(slot(g, co), g, co, 3).start()

    def complete(g):
        for kind, dc in ((0, 0), (1, 3), (2, 1), (3, 2)):
            c = ((x + dc) % 4) * 2 + 1 - core
            forward(slot(g, c), g, c, kind).wait_recv()

    def project(p, s):
        kk_s[s][...] = dot(all_a[p, 0:LIVE, :], w_s[3]).astype(BF16)
        fill_queries(qm_s[s], own_a[p], w_s[0])

    def logits(p, s):
        vt_s[s][...] = dot(w_s[4], all_a[p, 0:LIVE, :], 1, 1).astype(BF16)
        for t in range(3):
            lanes = slice(t * 256, t * 256 + 256)
            qm = qm_s[s][lanes, :]
            total = jnp.zeros((8, 256), F32)
            for k0 in range(0, LIVE, CHUNK):
                keys = slice(k0, k0 + CHUNK)
                e = jnp.exp(dot(kk_s[s][keys, :], qm, 1, 1) + bias_of(bias_s, t, k0, CHUNK))
                total = total + jnp.sum(e.reshape(CHUNK // 8, 8, 256), axis=0)
                p_s[s][keys, lanes] = e.astype(BF16)
            sum_s[s][:, lanes] = total

    def combine(s, live):
        outs = []
        for t in range(3):
            lanes = slice(t * 256, t * 256 + 256)
            r0, r1 = TILE_ROWS[t]
            o = dot(vt_s[s][r0:r1, :], p_s[s][:, lanes])
            total = jnp.sum(sum_s[s][:, lanes], axis=0, keepdims=True)
            o_max = jnp.max(jnp.abs(o), axis=0, keepdims=True)
            good = (total > 1e-12) & (total < 1e25) & (o_max < 1e35)
            bad_s[0:1, lanes] = jnp.maximum(bad_s[0:1, lanes], jnp.where(good, 0.0, live))
            outs.append(o * (1.0 / total))
        o_s[s][...] = assemble(outs)

    relayed(0)
    relayed(1)
    complete(0)
    project(0, 0)

    def body(m, carry):
        @pl.when(jnp.logical_and(m % 2 == 0, jnp.logical_and(m >= 2, m <= 8)))
        def _():
            relayed(m // 2 + 1)

        @pl.when(jnp.logical_and(m % 2 == 1, m <= 9))
        def _():
            complete((m + 1) // 2)

        for s in range(2):
            i = 2 * m + s
            live = jnp.where((i >= 1) & (i <= PAIRS), 1.0, 0.0)
            done = jnp.clip(i - 2, 0, PAIRS - 1)
            write_rows(done, own_a[done], o_s[s][...], w_s, z_ref, out_ref)
            combine(1 - s, live)
            logits(jnp.minimum(i, PAIRS - 1), s)
            project(jnp.minimum(i + 1, PAIRS - 1), 1 - s)
        return carry

    lax.fori_loop(0, PAIRS // 2 + 1, body, 0)
    outs = [
        pltpu.make_async_copy(out_ref, out_hbm, out_sems.at[1]),
        pltpu.make_async_copy(all_a, all_a_hbm, out_sems.at[2]),
        pltpu.make_async_copy(bad_s, bad_hbm, out_sems.at[3]),
    ]
    for copy in outs:
        copy.start()

    for c in range(2):
        @pl.when(jnp.logical_and(core == c, jnp.logical_not(swap_self)))
        def _():
            bias1(c).wait_send()

    @pl.when(is_relay)
    def _():
        for step in range(1, 16):
            bias2(step, row).wait_send()

    for g in range(GROUPS):
        direct(own(g), g, col, 0).wait_send()
        direct(own(g), g, col, 1).wait_send()
        relay(g, co, 0).wait_send()
        for kind in range(4):
            forward(own(g), g, col, kind).wait_send()
    for copy in outs:
        copy.wait()
    b_out.wait()


def fused_call(z_t, gamma, beta, wb_t, mask, wq, wk, wv, wg, wo):
    dma = pltpu.SemaphoreType.DMA
    args = (z_t, gamma, beta, wb_t, mask, wq, wk, wv, wg, wo)
    two = lambda *spec: [pltpu.VMEM(*spec)] * 2
    return pl.pallas_call(
        fused_kernel,
        out_shape=(
            jax.ShapeDtypeStruct(z_t.shape, BF16),
            jax.ShapeDtypeStruct((PAIRS, KEYS, 128), BF16),
            jax.ShapeDtypeStruct((2, 8, 144, 128), BF16),
            jax.ShapeDtypeStruct((8, KEYS), F32),
        ),
        in_specs=[pl.BlockSpec(memory_space=pl.ANY)] * len(args),
        out_specs=(pl.BlockSpec(memory_space=pl.ANY),) * 4,
        scratch_shapes=[
            *[pltpu.VMEM(s.shape, s.dtype) for s in args],
            dma((13,)),
            pltpu.VMEM((PAIRS, COLS, 128), BF16),
            pltpu.VMEM((144, 128), BF16),
            pltpu.VMEM((PAIRS, KEYS, 128), BF16),
            pltpu.VMEM((2, 8, 144, 128), BF16),
            pltpu.VMEM(z_t.shape, BF16),
            pltpu.VMEM((COLS, 192), F32),
            pltpu.VMEM((KEYS, 384), F32),
            pltpu.VMEM((5, 128, 128), BF16),
            *two((LIVE, 128), BF16),
            *two((128, LIVE), BF16),
            *two((KEYS, 128), BF16),
            *two((LIVE, KEYS), BF16),
            *two((8, KEYS), F32),
            *two((128, COLS), F32),
            pltpu.VMEM((8, KEYS), F32),
            dma(()), dma((2,)), dma((16,)), dma((2, 4)),
            dma((2, GROUPS)), dma((2, GROUPS)), dma((GROUPS,)), dma((GROUPS,)), dma((4, GROUPS)), dma((4, GROUPS)),
            dma((4,)),
        ],
        compiler_params=pltpu.CompilerParams(collective_id=0, has_side_effects=True),
        cost_estimate=pl.CostEstimate(flops=10**11, bytes_accessed=10**9, transcendentals=14 * 10**6),
        name="fused",
    )(*args)


def shifted_kernel(
    bad_ref, y_in, all_a_hbm, all_b_hbm, z_hbm, mask_hbm, wq_hbm, wk_hbm, wv_hbm, wg_hbm, wo_hbm,
    y_out,
    all_a, all_b, z_ref, mask_ref, wq_ref, wk_ref, wv_ref, wg_ref, wo_ref, sems,
    bias_s, w_s, kk, vt, qm, p_s, l_s, out_ref,
):
    @pl.when(jnp.max(bad_ref[...]) > 0.0)
    def _():
        col = lax.axis_index("col")
        for copy in load([
            (all_a_hbm, all_a), (all_b_hbm, all_b), (z_hbm, z_ref), (mask_hbm, mask_ref), (wq_hbm, wq_ref),
            (wk_hbm, wk_ref), (wv_hbm, wv_ref), (wg_hbm, wg_ref), (wo_hbm, wo_ref)], sems):
            copy.wait()
        fill_weights(w_s, wq_ref, wk_ref, wv_ref, wg_ref, wo_ref)
        fill_bias(bias_s, all_b, mask_ref)

        def body(p, carry):
            own = all_a[p, pl.ds(pl.multiple_of(col * COLS, COLS), COLS), :]
            kk[...] = dot(all_a[p], w_s[3]).astype(BF16)
            vt[...] = dot(w_s[4], all_a[p], 1, 1).astype(BF16)
            fill_queries(qm, own, w_s[0])
            outs = []
            for t in range(3):
                lanes = slice(t * 256, t * 256 + 256)
                peak = jnp.full((1, 256), -jnp.inf, F32)
                for k0 in range(0, KEYS, 128):
                    keys = slice(k0, k0 + 128)
                    s = dot(kk[keys, :], qm[lanes, :], 1, 1) + bias_of(bias_s, t, k0, 128)
                    l_s[keys, :] = s
                    peak = jnp.maximum(peak, jnp.max(s, axis=0, keepdims=True))
                total = jnp.zeros((1, 256), F32)
                for k0 in range(0, KEYS, 128):
                    keys = slice(k0, k0 + 128)
                    e = jnp.exp(l_s[keys, :] - peak)
                    total = total + jnp.sum(e, axis=0, keepdims=True)
                    p_s[keys, :] = e.astype(BF16)
                r0, r1 = TILE_ROWS[t]
                outs.append(dot(vt[r0:r1, :], p_s[...]) * (1.0 / total))
            write_rows(p, own, assemble(outs), w_s, z_ref, out_ref)
            return carry

        lax.fori_loop(0, PAIRS, body, 0)
        copy = pltpu.make_async_copy(out_ref, y_out, sems.at[0])
        copy.start()
        copy.wait()


def shifted_call(bad, y, all_a, all_b, z_t, mask, wq, wk, wv, wg, wo):
    args = (all_a, all_b, z_t, mask, wq, wk, wv, wg, wo)
    return pl.pallas_call(
        shifted_kernel,
        out_shape=jax.ShapeDtypeStruct(z_t.shape, BF16),
        in_specs=[pl.BlockSpec(memory_space=pltpu.VMEM)] + [pl.BlockSpec(memory_space=pl.ANY)] * (len(args) + 1),
        out_specs=pl.BlockSpec(memory_space=pl.ANY),
        input_output_aliases={1: 0},
        scratch_shapes=[
            *[pltpu.VMEM(s.shape, s.dtype) for s in args],
            pltpu.SemaphoreType.DMA((len(args),)),
            pltpu.VMEM((KEYS, 384), F32),
            pltpu.VMEM((5, 128, 128), BF16),
            pltpu.VMEM((KEYS, 128), BF16),
            pltpu.VMEM((128, KEYS), BF16),
            pltpu.VMEM((KEYS, 128), BF16),
            pltpu.VMEM((KEYS, 256), BF16),
            pltpu.VMEM((KEYS, 256), F32),
            pltpu.VMEM(z_t.shape, BF16),
        ],
        name="shifted",
    )(bad, y, *args)


def solution(mesh):
    tile_spec = P(("dp", "row"), "col", None)

    def per_device(pair_tile, res_mask, ln_gamma, ln_beta, w_q, w_k, w_v, w_b, w_g, w_o):
        z_t = jnp.transpose(pair_tile, (0, 2, 1))
        mask = res_mask.reshape(6, 128)
        y, all_a, all_b, bad = fused_call(
            z_t, ln_gamma.reshape(1, CH), ln_beta.reshape(1, CH), jnp.transpose(w_b), mask, w_q, w_k, w_v, w_g, w_o
        )
        y = shifted_call(bad, y, all_a, all_b, z_t, mask, w_q, w_k, w_v, w_g, w_o)
        return jnp.transpose(y, (0, 2, 1))

    return jax.shard_map(
        per_device, mesh=mesh,
        in_specs=(tile_spec, P("dp"), P(), P(), P(), P(), P(), P(), P(), P()),
        out_specs=tile_spec, check_vma=False,
    )
```

time: 226 us -> 56.2 us (0.25)
  the two profiles are of different devices: /device:TPU:0 before, /device:TPU:1 now
where the time goes in v2:
time: 56.2 us; the launch traced here: 56 us
  Pallas kernels  53.9 us (96%)
  local copies, waits for them, and re-layouts  2.06 us (4%)
    pallas_call x1, Pallas kernels, fused_call(): pl.pallas_call(fused_kernel, out_shape=(jax.ShapeDtypeStruct(z_t.shape, B...  53 us
    unnamed x1, local copies, waits for them, and re-layouts  2.06 us

profile of v2, /device:TPU:1, one launch (start us, length us, event | category | flops | bytes accessed | tf_op | source)
XLA Modules:
  0.0 56.0 jit_solution(9200790729750467394)
XLA Ops:
  0.0 53.0 %fused.1 = (bf16[48,64,96]{2,1,0:T(8,128)(2,1)}, bf16[24,768,128]{2,1,0:T(8,128)(2,1)}, bf16[2,8,144,128]{3,2,1,0:T(8,128)(2,1)}, f32[8,768]{1,0:T(8,128)}) custom-call(bf16[48,64,96]{2,1,0:T(8,128)(2,1)} %bitcast.7, f32[1,64]{1,0:T(1,128)} %bitcast.12, f32[1,64]{1,0:T(1,128)} %bitcast.13, bf16[4,64]{1,0:T(4,128)(2,1)} %bitcast.11, s32[6,128]{1,0:T(8,128)} %bitcast.9, ...), custom_call_target="tpu_custom_call" | custom-call | flops 99999997952 | bytes 1000000000 | tf_op jit(solution)/shard_map/fused/pallas_call | solution.py:391
  53.0 0.9 %shifted.1 = bf16[48,64,96]{2,1,0:T(8,128)(2,1)} custom-call(f32[8,768]{1,0:T(8,128)} %get-tuple-element.9.bad_ref, bf16[48,64,96]{2,1,0:T(8,128)(2,1)} %get-tuple-element.10.y_in, bf16[24,768,128]{2,1,0:T(8,128)(2,1)} %get-tuple-element.11.all_a_hbm, bf16[2,8,144,128]{3,2,1,0:T(8,128)(2,1)} %get-tuple-element.12.all_b_hbm, ...), custom_call_target="tpu_custom_call", output_to_operand_aliasing={{}: (1, {})} | custom-call | tf_op jit(solution)/shard_map/shifted/pallas_call | solution.py:478
  54.0 2.1 %copy.14 = bf16[48,96,64]{1,2,0:T(8,128)(2,1)} copy(bf16[48,96,64]{1,2,0:T(8,128)(2,1)} %bitcast.6) | data formatting | bytes 1179648

commit v3 on v2

--- a/solution.py
+++ b/solution.py
@@ -17,9 +17,10 @@
 HEADS, HEAD = 4, 16
 KEYS = 768
 BLOCKS = 8
-GROUPS, GP = 6, 4
+GROUPS, GP = 12, 2
+LEAD = 4
 LIVE = 672
-CHUNK = 112
+CHUNK = 336
 TILE_ROWS = ((0, 48), (32, 96), (80, 128))
 
 
@@ -51,17 +52,17 @@
 
 
 def fill_weights(w_s, wq_ref, wk_ref, wv_ref, wg_ref, wo_ref):
-    w_s[0] = block_diag(wq_ref[...])
+    w_s[0] = jnp.transpose(block_diag(wq_ref[...]).astype(F32)).astype(BF16)
     w_s[1] = jnp.transpose(block_diag(wg_ref[...]).astype(F32)).astype(BF16)
     w_s[2] = jnp.transpose(block_diag(wo_ref[...]).astype(F32)).astype(BF16)
     w_s[3] = block_diag(wk_ref[...])
     w_s[4] = jnp.transpose(block_diag(wv_ref[...]).astype(F32)).astype(BF16)
 
 
-def fill_bias(bias_s, all_b, mask_ref):
+def fill_bias(bias_s, all_b, mask_ref, blocks=range(8)):
     length = jnp.sum((mask_ref[...] > 0).astype(F32), axis=1, keepdims=True)
     length = jnp.sum(length, axis=0, keepdims=True)
-    for c in range(8):
+    for c in blocks:
         tiles = []
         for par in range(2):
             t = all_b[par, c].astype(F32)
@@ -81,11 +82,10 @@
     return jnp.concatenate([bias_s[k0:k0 + nk, 256:384], bias_s[k0:k0 + nk, 0:128]], axis=1)
 
 
-def fill_queries(qm, own, wq):
-    q = dot(own, wq) * HEAD ** -0.5
-    block = iota((COLS, 128), 1) // HEAD
+def fill_queries(qm, own, wq_t):
+    q = (dot(wq_t, own, 1, 1) * HEAD ** -0.5).astype(BF16)
     for b in range(BLOCKS):
-        qm[b * COLS:(b + 1) * COLS, :] = jnp.where(block == b, q, 0.0).astype(BF16)
+        qm[b * HEAD:(b + 1) * HEAD, b * COLS:(b + 1) * COLS] = q[b * HEAD:(b + 1) * HEAD, :]
 
 
 def assemble(o_tiles):
@@ -226,9 +226,13 @@
             device_id=partner, device_id_type=MESH,
         )
 
-    for g in range(GROUPS):
+    def send_direct(g):
         direct(own(g), g, col, 0).start()
         direct(own(g), g, col, 1).start()
+
+    for g in range(LEAD):
+        send_direct(g)
+    for g in range(GROUPS):
         forward(own(g), g, col, 0).start()
 
     @pl.when(swap_self)
@@ -239,6 +243,8 @@
     for copy in copies[7:]:
         copy.wait()
     fill_weights(w_s, wq_ref, wk_ref, wv_ref, wg_ref, wo_ref)
+    for qm in qm_s:
+        qm[...] = jnp.zeros_like(qm)
 
     def peak(ref):
         return jnp.max(jnp.max(jnp.abs(ref[...].astype(F32)), axis=1, keepdims=True), axis=0, keepdims=True)
@@ -255,31 +261,74 @@
             device_id={"row": (row + step) % 16, "col": col}, device_id_type=MESH,
         )
 
-    @pl.when(is_relay)
-    def _():
-        for c in range(2):
-            @pl.when(jnp.logical_not(jnp.logical_and(z == x, core == c)))
-            def _():
-                pltpu.make_async_remote_copy(
-                    src_ref=own_b, dst_ref=all_b.at[y % 2, 2 * z + c], send_sem=send_b1, recv_sem=recv_b1.at[c],
-                    device_id=swap, device_id_type=MESH,
-                ).wait_recv()
-        for step in range(1, 16):
-            bias2(step, row).start()
+    def bias_relay():
+        @pl.when(is_relay)
+        def _():
+            for c in range(2):
+                @pl.when(jnp.logical_not(jnp.logical_and(z == x, core == c)))
+                def _():
+                    pltpu.make_async_remote_copy(
+                        src_ref=own_b, dst_ref=all_b.at[y % 2, 2 * z + c], send_sem=send_b1,
+                        recv_sem=recv_b1.at[c], device_id=swap, device_id_type=MESH,
+                    ).wait_recv()
+            for step in range(1, 16):
+                bias2(step, row).start()
 
     cl, cr, co = ((x + 3) % 4) * 2 + core, ((x + 1) % 4) * 2 + core, ((x + 2) % 4) * 2 + core
-    for g in range(GROUPS):
+
+    def event(g):
         direct(slot(g, cl), g, cl, 0).wait_recv()
-        if g % 2 == 0:
+
+        @pl.when(g % 2 == 0)
+        def _():
             relay(g, cl, 0).start()
+
         forward(slot(g, cl), g, cl, 1).start()
         direct(slot(g, cr), g, cr, 1).wait_recv()
-        if g % 2 == 1:
+
+        @pl.when(g % 2 == 1)
+        def _():
             relay(g, cr, 1).start()
+
         forward(slot(g, cr), g, cr, 2).start()
 
-    for sy in range(2):
-        for sz in range(4):
+        @pl.when(g < GROUPS - LEAD)
+        def _():
+            send_direct(g + LEAD)
+
+    def relayed(g):
+        relay(g, co, 0).wait_recv()
+        forward(slot(g, co), g, co, 3).start()
+
+    def complete(g):
+        for kind, dc in ((0, 0), (1, 3), (2, 1), (3, 2)):
+            c = ((x + dc) % 4) * 2 + 1 - core
+            forward(slot(g, c), g, c, kind).wait_recv()
+
+    def early(g, carry):
+        event(g)
+
+        @pl.when(g == 1)
+        def _():
+            bias_relay()
+
+        @pl.when(g >= 2)
+        def _():
+            relayed(g - 2)
+
+        return carry
+
+    lax.fori_loop(0, 8, early, 0)
+
+    def project(p, s):
+        kk_s[s][...] = dot(all_a[p, 0:LIVE, :], w_s[3]).astype(BF16)
+        fill_queries(qm_s[s], own_a[p], w_s[0])
+
+    complete(0)
+    project(0, 0)
+
+    for sz in range(4):
+        for sy in range(2):
             @pl.when(jnp.logical_not(row == sz * 4 + 2 * core + sy))
             def _():
                 ref = all_b.at[sy, pl.ds(2 * sz, 2)]
@@ -287,77 +336,79 @@
                     src_ref=ref, dst_ref=ref, send_sem=send_b2.at[1], recv_sem=recv_b2.at[sy, sz],
                     device_id=partner, device_id_type=MESH,
                 ).wait_recv()
-    fill_bias(bias_s, all_b, mask_ref)
+        fill_bias(bias_s, all_b, mask_ref, (2 * sz, 2 * sz + 1))
     b_out = pltpu.make_async_copy(all_b, all_b_hbm, out_sems.at[0])
     b_out.start()
 
-    def relayed(g):
-        relay(g, co, 0).wait_recv()
-        forward(slot(g, co), g, co, 3).start()
-
-    def complete(g):
-        for kind, dc in ((0, 0), (1, 3), (2, 1), (3, 2)):
-            c = ((x + dc) % 4) * 2 + 1 - core
-            forward(slot(g, c), g, c, kind).wait_recv()
-
-    def project(p, s):
-        kk_s[s][...] = dot(all_a[p, 0:LIVE, :], w_s[3]).astype(BF16)
-        fill_queries(qm_s[s], own_a[p], w_s[0])
-
-    def logits(p, s):
+    def values(p, s):
         vt_s[s][...] = dot(w_s[4], all_a[p, 0:LIVE, :], 1, 1).astype(BF16)
-        for t in range(3):
-            lanes = slice(t * 256, t * 256 + 256)
-            qm = qm_s[s][lanes, :]
-            total = jnp.zeros((8, 256), F32)
-            for k0 in range(0, LIVE, CHUNK):
-                keys = slice(k0, k0 + CHUNK)
-                e = jnp.exp(dot(kk_s[s][keys, :], qm, 1, 1) + bias_of(bias_s, t, k0, CHUNK))
-                total = total + jnp.sum(e.reshape(CHUNK // 8, 8, 256), axis=0)
-                p_s[s][keys, lanes] = e.astype(BF16)
-            sum_s[s][:, lanes] = total
-
-    def combine(s, live):
-        outs = []
-        for t in range(3):
-            lanes = slice(t * 256, t * 256 + 256)
-            r0, r1 = TILE_ROWS[t]
-            o = dot(vt_s[s][r0:r1, :], p_s[s][:, lanes])
-            total = jnp.sum(sum_s[s][:, lanes], axis=0, keepdims=True)
-            o_max = jnp.max(jnp.abs(o), axis=0, keepdims=True)
-            good = (total > 1e-12) & (total < 1e25) & (o_max < 1e35)
-            bad_s[0:1, lanes] = jnp.maximum(bad_s[0:1, lanes], jnp.where(good, 0.0, live))
-            outs.append(o * (1.0 / total))
-        o_s[s][...] = assemble(outs)
-
-    relayed(0)
-    relayed(1)
-    complete(0)
-    project(0, 0)
+
+    def logits(s, t):
+        lanes = slice(t * 256, t * 256 + 256)
+        qm = qm_s[s][:, lanes]
+        total = jnp.zeros((8, 256), F32)
+        for k0 in range(0, LIVE, CHUNK):
+            keys = slice(k0, k0 + CHUNK)
+            e = jnp.exp(dot(kk_s[s][keys, :], qm) + bias_of(bias_s, t, k0, CHUNK))
+            total = total + jnp.sum(e.reshape(CHUNK // 8, 8, 256), axis=0)
+            p_s[s][keys, lanes] = e.astype(BF16)
+        sum_s[s][:, lanes] = total
+
+    def combine(s, t, live):
+        lanes = slice(t * 256, t * 256 + 256)
+        r0, r1 = TILE_ROWS[t]
+        o = dot(vt_s[s][r0:r1, :], p_s[s][:, lanes])
+        total = jnp.sum(sum_s[s][:, lanes], axis=0, keepdims=True)
+        o_max = jnp.max(jnp.abs(o), axis=0, keepdims=True)
+        good = (total > 1e-12) & (total < 1e25) & (o_max < 1e35)
+        bad_s[0:1, lanes] = jnp.maximum(bad_s[0:1, lanes], jnp.where(good, 0.0, live))
+        return o * (1.0 / total)
+
+
+    a_out = pltpu.make_async_copy(all_a, all_a_hbm, out_sems.at[2])
 
     def body(m, carry):
-        @pl.when(jnp.logical_and(m % 2 == 0, jnp.logical_and(m >= 2, m <= 8)))
-        def _():
-            relayed(m // 2 + 1)
-
-        @pl.when(jnp.logical_and(m % 2 == 1, m <= 9))
-        def _():
-            complete((m + 1) // 2)
+        @pl.when(m <= 3)
+        def _():
+            event(8 + m)
+
+        @pl.when(m <= 5)
+        def _():
+            relayed(6 + m)
+
+        @pl.when(m <= 10)
+        def _():
+            complete(m + 1)
+
+        @pl.when(m == 11)
+        def _():
+            a_out.start()
 
         for s in range(2):
             i = 2 * m + s
-            live = jnp.where((i >= 1) & (i <= PAIRS), 1.0, 0.0)
-            done = jnp.clip(i - 2, 0, PAIRS - 1)
+            live = jnp.where(i >= 1, 1.0, 0.0)
+            done = jnp.maximum(i - 2, 0)
+            logits(s, 0)
+            o_0 = combine(1 - s, 0, live)
+            values(i, s)
+            logits(s, 1)
+            o_1 = combine(1 - s, 1, live)
+            project(jnp.minimum(i + 1, PAIRS - 1), 1 - s)
+            logits(s, 2)
+            o_2 = combine(1 - s, 2, live)
+            o_s[1 - s][...] = assemble([o_0, o_1, o_2])
             write_rows(done, own_a[done], o_s[s][...], w_s, z_ref, out_ref)
-            combine(1 - s, live)
-            logits(jnp.minimum(i, PAIRS - 1), s)
-            project(jnp.minimum(i + 1, PAIRS - 1), 1 - s)
         return carry
 
-    lax.fori_loop(0, PAIRS // 2 + 1, body, 0)
+    lax.fori_loop(0, PAIRS // 2, body, 0)
+    tail = 2 * PAIRS - 4
+    head_out = pltpu.make_async_copy(out_ref.at[0:tail], out_hbm.at[0:tail], out_sems.at[4])
+    head_out.start()
+    write_rows(PAIRS - 2, own_a[PAIRS - 2], o_s[0][...], w_s, z_ref, out_ref)
+    o_s[1][...] = assemble([combine(1, t, 1.0) for t in range(3)])
+    write_rows(PAIRS - 1, own_a[PAIRS - 1], o_s[1][...], w_s, z_ref, out_ref)
     outs = [
-        pltpu.make_async_copy(out_ref, out_hbm, out_sems.at[1]),
-        pltpu.make_async_copy(all_a, all_a_hbm, out_sems.at[2]),
+        pltpu.make_async_copy(out_ref.at[tail:2 * PAIRS], out_hbm.at[tail:2 * PAIRS], out_sems.at[1]),
         pltpu.make_async_copy(bad_s, bad_hbm, out_sems.at[3]),
     ]
     for copy in outs:
@@ -381,7 +432,9 @@
             forward(own(g), g, col, kind).wait_send()
     for copy in outs:
         copy.wait()
+    a_out.wait()
     b_out.wait()
+    head_out.wait()
 
 
 def fused_call(z_t, gamma, beta, wb_t, mask, wq, wk, wv, wg, wo):
@@ -411,14 +464,14 @@
             pltpu.VMEM((5, 128, 128), BF16),
             *two((LIVE, 128), BF16),
             *two((128, LIVE), BF16),
-            *two((KEYS, 128), BF16),
+            *two((128, KEYS), BF16),
             *two((LIVE, KEYS), BF16),
             *two((8, KEYS), F32),
             *two((128, COLS), F32),
             pltpu.VMEM((8, KEYS), F32),
             dma(()), dma((2,)), dma((16,)), dma((2, 4)),
             dma((2, GROUPS)), dma((2, GROUPS)), dma((GROUPS,)), dma((GROUPS,)), dma((4, GROUPS)), dma((4, GROUPS)),
-            dma((4,)),
+            dma((5,)),
         ],
         compiler_params=pltpu.CompilerParams(collective_id=0, has_side_effects=True),
         cost_estimate=pl.CostEstimate(flops=10**11, bytes_accessed=10**9, transcendentals=14 * 10**6),
@@ -441,6 +494,7 @@
             copy.wait()
         fill_weights(w_s, wq_ref, wk_ref, wv_ref, wg_ref, wo_ref)
         fill_bias(bias_s, all_b, mask_ref)
+        qm[...] = jnp.zeros_like(qm)
 
         def body(p, carry):
             own = all_a[p, pl.ds(pl.multiple_of(col * COLS, COLS), COLS), :]
@@ -453,7 +507,7 @@
                 peak = jnp.full((1, 256), -jnp.inf, F32)
                 for k0 in range(0, KEYS, 128):
                     keys = slice(k0, k0 + 128)
-                    s = dot(kk[keys, :], qm[lanes, :], 1, 1) + bias_of(bias_s, t, k0, 128)
+                    s = dot(kk[keys, :], qm[:, lanes]) + bias_of(bias_s, t, k0, 128)
                     l_s[keys, :] = s
                     peak = jnp.maximum(peak, jnp.max(s, axis=0, keepdims=True))
                 total = jnp.zeros((1, 256), F32)
@@ -488,7 +542,7 @@
             pltpu.VMEM((5, 128, 128), BF16),
             pltpu.VMEM((KEYS, 128), BF16),
             pltpu.VMEM((128, KEYS), BF16),
-            pltpu.VMEM((KEYS, 128), BF16),
+            pltpu.VMEM((128, KEYS), BF16),
             pltpu.VMEM((KEYS, 256), BF16),
             pltpu.VMEM((KEYS, 256), F32),
             pltpu.VMEM(z_t.shape, BF16),

time: 56.2 us -> 50.9 us (0.906)
  Pallas kernels: 53.9 us -> 48.2 us
    pallas_call x1, Pallas kernels: 53 us -> 47.3 us  [fused_call(): pl.pallas_call(fused_kernel, out_shape=(jax.ShapeDtypeStruct(z_t.shape, B...]
where the time goes in v3:
time: 50.9 us; the launch traced here: 50.3 us
  Pallas kernels  48.2 us (95%)
  local copies, waits for them, and re-layouts  2.06 us (4%)
    pallas_call x1, Pallas kernels, fused_call(): pl.pallas_call(fused_kernel, out_shape=(jax.ShapeDtypeStruct(z_t.shape, B...  47.3 us
    unnamed x1, local copies, waits for them, and re-layouts  2.06 us

profile of v3, /device:TPU:1, one launch (start us, length us, event | category | flops | bytes accessed | tf_op | source)
XLA Modules:
  0.0 50.3 jit_solution(1436204065894546571)
XLA Ops:
  0.0 47.3 %fused.1 = (bf16[48,64,96]{2,1,0:T(8,128)(2,1)}, bf16[24,768,128]{2,1,0:T(8,128)(2,1)}, bf16[2,8,144,128]{3,2,1,0:T(8,128)(2,1)}, f32[8,768]{1,0:T(8,128)}) custom-call(bf16[48,64,96]{2,1,0:T(8,128)(2,1)} %bitcast.7, f32[1,64]{1,0:T(1,128)} %bitcast.12, f32[1,64]{1,0:T(1,128)} %bitcast.13, bf16[4,64]{1,0:T(4,128)(2,1)} %bitcast.11, s32[6,128]{1,0:T(8,128)} %bitcast.9, ...), custom_call_target="tpu_custom_call" | custom-call | flops 99999997952 | bytes 1000000000 | tf_op jit(solution)/shard_map/fused/pallas_call | solution.py:444
  47.3 0.9 %shifted.1 = bf16[48,64,96]{2,1,0:T(8,128)(2,1)} custom-call(f32[8,768]{1,0:T(8,128)} %get-tuple-element.9.bad_ref, bf16[48,64,96]{2,1,0:T(8,128)(2,1)} %get-tuple-element.10.y_in, bf16[24,768,128]{2,1,0:T(8,128)(2,1)} %get-tuple-element.11.all_a_hbm, bf16[2,8,144,128]{3,2,1,0:T(8,128)(2,1)} %get-tuple-element.12.all_b_hbm, ...), custom_call_target="tpu_custom_call", output_to_operand_aliasing={{}: (1, {})} | custom-call | tf_op jit(solution)/shard_map/shifted/pallas_call | solution.py:532
  48.3 2.1 %copy.14 = bf16[48,96,64]{1,2,0:T(8,128)(2,1)} copy(bf16[48,96,64]{1,2,0:T(8,128)(2,1)} %bitcast.6) | data formatting | bytes 1179648
